TPU v7x, 32 devices: a 4x2x2 block of a 4x4x8 slice. The times are simulated.
32 devices in a mesh: dp: 4 (over y, z), sp: 8 (over x, core).
Axes of the slice: x: 4, y: 2, z: 2, core: 2. Of those that a mesh axis runs over, the one named last changes fastest.
The devices are a block of a 4x4x8 slice.
Arguments:
- hidden: bfloat16 [4096, 2048], P(('dp', 'sp')), parts along dimension 0
- ln_gain: bfloat16 [2048], replicated
- w_q: bfloat16 [2048, 4096], replicated
- w_k: bfloat16 [2048, 512], replicated
- w_v: bfloat16 [2048, 512], replicated
- w_o: bfloat16 [4096, 2048], replicated
- q_gain: bfloat16 [128], replicated
- k_gain: bfloat16 [128], replicated
Outputs:
- output: bfloat16 [4096, 2048], P(('dp', 'sp')), parts along dimension 0
There are 4 independent parts. A program takes and returns all parts, laid end to end along the dimension named above; an argument that names none is the same for every part.
All inputs are finite; a program needn't handle non-finite values.
Results may differ from a plain program's by a relative error of at most 0.00713517.
Values are sent between devices in bfloat16 or wider.
A program may use at most 768 MiB of HBM per device.

v0:
```python
import jax
import jax.numpy as jnp
from jax import lax
from jax.sharding import PartitionSpec as P

EPS = 1e-6
THETA = 1000000.0


def head_norm(values, gain):
    return values * lax.rsqrt(jnp.mean(values * values, axis=-1, keepdims=True) + EPS) * gain.astype(jnp.float32)


def rotate(values, positions):
    head_dim = values.shape[-1]
    half = head_dim // 2
    inv_freq = jnp.power(THETA, -(jnp.arange(half, dtype=jnp.float32) * (2.0 / head_dim)))
    angles = positions.astype(jnp.float32)[:, None] * inv_freq[None, :]
    cos_pos = jnp.cos(angles)[:, None, :]
    sin_pos = jnp.sin(angles)[:, None, :]
    first_half = values[..., :half]
    second_half = values[..., half:]
    return jnp.concatenate([first_half * cos_pos - second_half * sin_pos, second_half * cos_pos + first_half * sin_pos], axis=-1)


def project(hidden, ln_gain, w_q, w_k, w_v, q_gain, k_gain, positions):
    tokens = hidden.shape[0]
    head_dim = q_gain.shape[0]
    hidden_f32 = hidden.astype(jnp.float32)
    normed = (hidden_f32 * lax.rsqrt(jnp.mean(hidden_f32 * hidden_f32, axis=-1, keepdims=True) + EPS) * ln_gain.astype(jnp.float32)).astype(jnp.bfloat16)
    q_raw = jnp.dot(normed, w_q, preferred_element_type=jnp.float32).reshape(tokens, -1, head_dim)
    k_raw = jnp.dot(normed, w_k, preferred_element_type=jnp.float32).reshape(tokens, -1, head_dim)
    v_local = jnp.dot(normed, w_v, preferred_element_type=jnp.float32).astype(jnp.bfloat16).reshape(tokens, -1, head_dim)
    q_local = rotate(head_norm(q_raw, q_gain), positions).astype(jnp.bfloat16)
    k_local = rotate(head_norm(k_raw, k_gain), positions).astype(jnp.bfloat16)
    return hidden_f32, q_local, k_local, v_local


def attend(q_all, k_all, v_all, q_start):
    q_rows, q_heads, head_dim = q_all.shape
    k_rows = k_all.shape[0]
    k_heads = k_all.shape[1]
    group = q_heads // k_heads
    limit = 2 ** 25 // (q_heads * k_rows)
    block_rows = min(q_rows, 2 ** max(3, min(9, limit.bit_length() - 1)))
    num_blocks = q_rows // block_rows
    q_blocks = q_all.reshape(num_blocks, block_rows, k_heads, group, head_dim)
    key_pos = jnp.arange(k_rows)
    score_scale = head_dim ** -0.5

    def one_block(block_args):
        q_block, block_idx = block_args
        scores = jnp.einsum('qkgd,skd->kgqs', q_block, k_all, preferred_element_type=jnp.float32) * score_scale
        q_pos = q_start + block_idx * block_rows + jnp.arange(block_rows)
        visible = q_pos[:, None] >= key_pos[None, :]
        scores = jnp.where(visible, scores, -jnp.inf)
        attn_prob = jax.nn.softmax(scores, axis=-1).astype(jnp.bfloat16)
        mixed = jnp.einsum('kgqs,skd->qkgd', attn_prob, v_all, preferred_element_type=jnp.float32)
        return mixed.astype(jnp.bfloat16)

    outputs = lax.map(one_block, (q_blocks, jnp.arange(num_blocks)))
    return outputs.reshape(q_rows, q_heads, head_dim)


def finish(hidden_f32, mixed, w_o):
    tokens = mixed.shape[0]
    result = hidden_f32 + jnp.dot(mixed.reshape(tokens, -1), w_o, preferred_element_type=jnp.float32)
    return result.astype(jnp.bfloat16)


def solution(mesh):
    group_size = mesh.shape['sp']

    def device_step(hidden, ln_gain, w_q, w_k, w_v, w_o, q_gain, k_gain):
        tokens = hidden.shape[0]
        head_dim = q_gain.shape[0]
        kv_heads = w_k.shape[1] // head_dim
        copies = max(1, group_size // kv_heads)
        positions = lax.axis_index('sp') * tokens + jnp.arange(tokens)
        hidden_f32, q_local, k_local, v_local = project(hidden, ln_gain, w_q, w_k, w_v, q_gain, k_gain, positions)
        q_heads = lax.all_to_all(q_local, 'sp', 1, 0, tiled=True)
        k_heads = lax.all_to_all(jnp.repeat(k_local, copies, axis=1), 'sp', 1, 0, tiled=True)
        v_heads = lax.all_to_all(jnp.repeat(v_local, copies, axis=1), 'sp', 1, 0, tiled=True)
        mixed = attend(q_heads, k_heads, v_heads, 0)
        mixed_local = lax.all_to_all(mixed, 'sp', 0, 1, tiled=True)
        return finish(hidden_f32, mixed_local, w_o)

    row_spec = P(('dp', 'sp'), None)
    return jax.shard_map(device_step, mesh=mesh, in_specs=(row_spec, P(), P(), P(), P(), P(), P(), P()), out_specs=row_spec, check_vma=False)
```

profile of v0, /device:TPU:81, one launch (start us, length us, event | category | flops | bytes accessed | tf_op | source)
XLA Modules:
  0.0 105.4 jit_solution(14791000328977183983)
XLA Ops:
  0.0 0.8 convert_element_type.47
  0.9 1.2 %fusion.26 = f32[128]{0:T(128)S(1)} fusion(bf16[128,2048]{1,0:T(8,128)(2,1)} %param.10), kind=kLoop, calls=%fused_computation.32 | loop fusion | flops 786304 | bytes 524800 | tf_op jit(solution)/shard_map/reduce_sum | solution.py:30
  2.1 1.5 %fusion.30 = f32[128,512]{1,0:T(8,128)S(1)} fusion(bf16[2048,512]{1,0:T(8,128)(2,1)S(1)} %copy-done, bf16[128,2048]{1,0:T(8,128)(2,1)} %param.10, f32[2048]{0:T(1024)S(1)} %convert_element_type.47, f32[128]{0:T(128)S(1)} %add_rsqrt_fusion.2), kind=kOutput, calls=%fused_computation.49 | convolution fusion | flops 269484032 | bytes 2892288 | tf_op jit(solution)/shard_map/dot_general | solution.py:32
  5.8 6.0 %all-to-all-start.1 = ((bf16[128,8,128]{2,0,1:T(8,128)(2,1)}), bf16[128,8,128]{2,0,1:T(8,128)(2,1)S(1)}, u32[]{:S(2)}, u32[]{:S(2)}) async-start(bf16[128,8,128]{2,0,1:T(8,128)(2,1)} %bitcast.3), calls=%async_computation.1 | async-start | bytes 524288 | tf_op jit(solution)/shard_map/all_to_all | solution.py:82
  11.8 8.2 %fusion.32 = f32[128,4096]{1,0:T(8,128)S(1)} fusion(bf16[2048,4096]{1,0:T(8,128)(2,1)} %param.12, bf16[128,2048]{1,0:T(8,128)(2,1)S(1)} %copy-done.2, f32[2048]{0:T(1024)S(1)} %convert_element_type.47, f32[128]{0:T(128)S(1)} %add_rsqrt_fusion.2), kind=kOutput, calls=%fused_computation.50 | convolution fusion | flops 2148532224 | bytes 19407360 | tf_op jit(solution)/shard_map/dot_general | solution.py:31
  22.7 1.6 %pad_maximum_fusion = bf16[128,32,128]{2,0,1:T(8,128)(2,1)} fusion(bf16[128,32,64]{2,0,1:T(8,128)(2,1)S(1)} %get-tuple-element.108, bf16[128,32,64]{2,0,1:T(8,128)(2,1)S(1)} %get-tuple-element.107), kind=kLoop, calls=%fused_computation.35 | loop fusion | flops 2097152 | bytes 2097152 | tf_op jit(solution)/shard_map/concatenate | solution.py:23
  24.2 4.8 %all-to-all-start = ((bf16[128,32,128]{2,0,1:T(8,128)(2,1)}), bf16[128,32,128]{2,0,1:T(8,128)(2,1)S(1)}, u32[]{:S(2)}, u32[]{:S(2)}) async-start(bf16[128,32,128]{2,0,1:T(8,128)(2,1)} %pad_maximum_fusion), calls=%async_computation | async-start | bytes 2097152 | tf_op jit(solution)/shard_map/all_to_all | solution.py:81
  29.1 2.1 %fusion.25 = bf16[16,4,8,128]{3,2,1,0:T(8,128)(2,1)S(1)} fusion(bf16[2048,512]{1,0:T(8,128)(2,1)} %param.14, bf16[128,2048]{1,0:T(8,128)(2,1)S(1)} %copy-done.2, f32[2048]{0:T(1024)S(1)} %convert_element_type.47, f32[128]{0:T(128)S(1)} %add_rsqrt_fusion.2), kind=kOutput, calls=%fused_computation.31 | convolution fusion | flops 269549568 | bytes 2761216 | tf_op jit(solution)/shard_map/dot_general | solution.py:33
  31.2 12.6 %all-to-all-done = bf16[128,32,128]{2,0,1:T(8,128)(2,1)S(1)} async-done(((bf16[128,32,128]{2,0,1:T(8,128)(2,1)}), bf16[128,32,128]{2,0,1:T(8,128)(2,1)S(1)}, u32[]{:S(2)}, u32[]{:S(2)}) %all-to-all-start) | async-done | bytes 1048608 | tf_op jit(solution)/shard_map/all_to_all | solution.py:81
  43.8 0.8 broadcast_in_dim.17
  44.6 4.5 %all-to-all-start.2 = ((bf16[128,8,128]{2,0,1:T(8,128)(2,1)}), bf16[128,8,128]{2,0,1:T(8,128)(2,1)S(1)}, u32[]{:S(2)}, u32[]{:S(2)}) async-start(bf16[128,8,128]{2,0,1:T(8,128)(2,1)} %bitcast.7), calls=%async_computation.2 | async-start | bytes 524288 | tf_op jit(solution)/shard_map/all_to_all | solution.py:83
  49.2 1.3 %copy.54 = bf16[8,128,4,128]{3,1,0,2:T(8,128)(2,1)S(1)} copy(bf16[8,128,4,128]{3,1,2,0:T(8,128)(2,1)} %bitcast.123) | data formatting | bytes 2097152 | tf_op jit(solution)/shard_map/all_to_all | solution.py:81
  50.5 5.1 %all-to-all-done.2 = bf16[128,8,128]{2,0,1:T(8,128)(2,1)S(1)} async-done(((bf16[128,8,128]{2,0,1:T(8,128)(2,1)}), bf16[128,8,128]{2,0,1:T(8,128)(2,1)S(1)}, u32[]{:S(2)}, u32[]{:S(2)}) %all-to-all-start.2) | async-done | bytes 262176 | tf_op jit(solution)/shard_map/all_to_all | solution.py:83
  55.5 18.4 %while.11 = (s32[]{:T(128)}, bf16[2,512,1,4,128]{4,1,0,3,2:T(8,128)(2,1)}, s32[2]{0:T(128)S(1)}, bf16[2,512,1,4,128]{4,1,0,3,2:T(8,128)(2,1)S(1)}, bf16[1024,1,1...) while((s32[]{:T(128)}, ...), condition=%wide.region_6.7_spmd.clone, body=%wide.region_3.6_spmd.clone.sunk | while | flops 1099690496 | bytes 28881524 | solution.py:61
  57.2 1.7 %fusion.47 = (f32[4,512]{1,0:T(4,128)S(1)}, f32[512,4,1024]{2,0,1:T(8,128)S(1)}) fusion(pred[512,1024]{1,0:T(8,128)(4,1)S(1)} %iota_compare_fusion.2, bf16[1024,1,128]{2,0,1:T(8,128)(2,1)S(1)} %get-tuple-element.174, bf16[2,512,1,4,128]{4,1,0,3,2:T(8,128)(2,1)S(1)} %get-tuple-element.173, s32[]{:T(128)} %get-tuple-element.162), kind=kOutput, calls=%fused_computation.5.clone.1 | convolution fusion | flops 543160320 | bytes 9707524 | tf_op jit(solution)/shard_map/while/body/eval_jaxpr/qkgd,skd->kgqs/dot_general | solution.py:53
  58.8 2.4 %fusion.48 = f32[4,512]{1,0:T(4,128)S(1)} fusion(f32[512,4,1024]{2,0,1:T(8,128)S(1)} %get-tuple-element.152, f32[4,512]{1,0:T(4,128)S(1)} %get-tuple-element.153, pred[512,1024]{1,0:T(8,128)(4,1)S(1)} %iota_compare_fusion.2), kind=kLoop, calls=%fused_computation.4.clone.1 | loop fusion | flops 8386560 | bytes 8929280 | tf_op jit(solution)/shard_map/while/body/eval_jaxpr/reduce_sum | solution.py:57
  61.3 3.5 %fusion.49 = bf16[2,512,1,4,128]{4,1,0,3,2:T(8,128)(2,1)} fusion(bf16[2,512,1,4,128]{4,1,0,3,2:T(8,128)(2,1)} %get-tuple-element.163, s32[]{:T(128)} %get-tuple-element.162, f32[4,512]{1,0:T(4,128)S(1)} %fusion.48, f32[4,512]{1,0:T(4,128)S(1)} %get-tuple-element.153, f32[512,4,1024]{2,0,1:T(8,128)S(1)} %get-tuple-element.152, ...), kind=kOutput, calls=%fused_computation.11.clone.1 | convolution fusion | flops 547618816 | bytes 9716224 | tf_op jit(solution)/shard_map/while/body/eval_jaxpr/kgqs,skd->qkgd/dot_general | solution.py:58
  66.4 1.7 %fusion.47 = (f32[4,512]{1,0:T(4,128)S(1)}, f32[512,4,1024]{2,0,1:T(8,128)S(1)}) fusion(pred[512,1024]{1,0:T(8,128)(4,1)S(1)} %iota_compare_fusion.2, bf16[1024,1,128]{2,0,1:T(8,128)(2,1)S(1)} %get-tuple-element.174, bf16[2,512,1,4,128]{4,1,0,3,2:T(8,128)(2,1)S(1)} %get-tuple-element.173, s32[]{:T(128)} %get-tuple-element.162), kind=kOutput, calls=%fused_computation.5.clone.1 | convolution fusion | flops 543160320 | bytes 9707524 | tf_op jit(solution)/shard_map/while/body/eval_jaxpr/qkgd,skd->kgqs/dot_general | solution.py:53
  68.0 2.4 %fusion.48 = f32[4,512]{1,0:T(4,128)S(1)} fusion(f32[512,4,1024]{2,0,1:T(8,128)S(1)} %get-tuple-element.152, f32[4,512]{1,0:T(4,128)S(1)} %get-tuple-element.153, pred[512,1024]{1,0:T(8,128)(4,1)S(1)} %iota_compare_fusion.2), kind=kLoop, calls=%fused_computation.4.clone.1 | loop fusion | flops 8386560 | bytes 8929280 | tf_op jit(solution)/shard_map/while/body/eval_jaxpr/reduce_sum | solution.py:57
  70.5 3.5 %fusion.49 = bf16[2,512,1,4,128]{4,1,0,3,2:T(8,128)(2,1)} fusion(bf16[2,512,1,4,128]{4,1,0,3,2:T(8,128)(2,1)} %get-tuple-element.163, s32[]{:T(128)} %get-tuple-element.162, f32[4,512]{1,0:T(4,128)S(1)} %fusion.48, f32[4,512]{1,0:T(4,128)S(1)} %get-tuple-element.153, f32[512,4,1024]{2,0,1:T(8,128)S(1)} %get-tuple-element.152, ...), kind=kOutput, calls=%fused_computation.11.clone.1 | convolution fusion | flops 547618816 | bytes 9716224 | tf_op jit(solution)/shard_map/while/body/eval_jaxpr/kgqs,skd->qkgd/dot_general | solution.py:58
  73.9 2.0 %copy.61 = bf16[1024,4,128]{2,1,0:T(4,128)(2,1)S(1)} copy(bf16[1024,4,128]{2,0,1:T(8,128)(2,1)} %bitcast.11) | data formatting | bytes 2097152 | tf_op jit(solution)/shard_map/reshape | solution.py:62
  76.0 18.6 %all_to_all.66 = bf16[1024,4,128]{2,1,0:T(4,128)(2,1)S(1)} all-to-all(bf16[1024,4,128]{2,1,0:T(4,128)(2,1)S(1)} %copy.61), channel_id=1, replica_groups=mesh['dp'=4,'sp'=8] {'sp'}, dimensions={0} | all-to-all | bytes 2097152 | tf_op jit(solution)/shard_map/all_to_all | solution.py:85
  94.7 1.3 %copy.63 = bf16[128,8,4,128]{0,3,2,1:T(8,128)(2,1)} copy(bf16[128,8,4,128]{3,0,1,2:T(8,128)(2,1)S(1)} %bitcast.124) | data formatting | bytes 2097152 | tf_op jit(solution)/shard_map/all_to_all | solution.py:85
  96.0 9.4 %fusion.23 = bf16[128,2048]{1,0:T(8,128)(2,1)} fusion(bf16[128,4096]{0,1:T(8,128)(2,1)} %bitcast.122, bf16[4096,2048]{1,0:T(8,128)(2,1)} %param.15, bf16[128,2048]{1,0:T(8,128)(2,1)S(1)} %copy-done.2), kind=kOutput, calls=%fused_computation.22 | convolution fusion | flops 2148270080 | bytes 18874368 | tf_op jit(solution)/shard_map/dot_general | solution.py:67
  (43 shorter events, 6.7 us)
Async XLA Ops:
  0.0 2.1 %copy-start = (bf16[2048,512]{1,0:T(8,128)(2,1)S(1)}, bf16[2048,512]{1,0:T(8,128)(2,1)}, u32[]{:S(2)}) copy-start(bf16[2048,512]{1,0:T(8,128)(2,1)} %param.13) | copy-start | bytes 6291460
  0.9 3.2 %copy-start.4 = (bf16[128]{0:T(256)(128)(2,1)S(1)}, bf16[128]{0:T(256)(128)(2,1)}, u32[]{:S(2)}) copy-start(bf16[128]{0:T(256)(128)(2,1)} %param.17) | copy-start | bytes 772
  3.7 8.2 %copy-start.2 = (bf16[128,2048]{1,0:T(8,128)(2,1)S(1)}, bf16[128,2048]{1,0:T(8,128)(2,1)}, u32[]{:S(2)}) copy-start(bf16[128,2048]{1,0:T(8,128)(2,1)} %param.10) | copy-start | bytes 1572868
  5.8 18.4 %all-to-all-start.1 = ((bf16[128,8,128]{2,0,1:T(8,128)(2,1)}), bf16[128,8,128]{2,0,1:T(8,128)(2,1)S(1)}, u32[]{:S(2)}, u32[]{:S(2)}) async-start(bf16[128,8,128]{2,0,1:T(8,128)(2,1)} %bitcast.3), calls=%async_computation.1 | async-start | bytes 524288 | tf_op jit(solution)/shard_map/all_to_all | solution.py:82
  20.4 0.7 copy-start.5
  24.2 19.6 %all-to-all-start = ((bf16[128,32,128]{2,0,1:T(8,128)(2,1)}), bf16[128,32,128]{2,0,1:T(8,128)(2,1)S(1)}, u32[]{:S(2)}, u32[]{:S(2)}) async-start(bf16[128,32,128]{2,0,1:T(8,128)(2,1)} %pad_maximum_fusion), calls=%async_computation | async-start | bytes 2097152 | tf_op jit(solution)/shard_map/all_to_all | solution.py:81
  43.8 5.3 %copy-start.3 = (bf16[128,32,128]{2,0,1:T(8,128)(2,1)}, bf16[128,32,128]{2,0,1:T(8,128)(2,1)S(1)}, u32[]{:S(2)}) copy-start(bf16[128,32,128]{2,0,1:T(8,128)(2,1)S(1)} %all-to-all-done) | copy-start | bytes 3145732
  44.6 10.9 %all-to-all-start.2 = ((bf16[128,8,128]{2,0,1:T(8,128)(2,1)}), bf16[128,8,128]{2,0,1:T(8,128)(2,1)S(1)}, u32[]{:S(2)}, u32[]{:S(2)}) async-start(bf16[128,8,128]{2,0,1:T(8,128)(2,1)} %bitcast.7), calls=%async_computation.2 | async-start | bytes 524288 | tf_op jit(solution)/shard_map/all_to_all | solution.py:83
  96.0 9.4 %copy-start.1 = (bf16[2048,512]{1,0:T(8,128)(2,1)S(1)}, bf16[2048,512]{1,0:T(8,128)(2,1)}, u32[]{:S(2)}) copy-start(bf16[2048,512]{1,0:T(8,128)(2,1)} %param.13) | copy-start | bytes 6291460
where the time goes:
time: 106 us; the launch traced here: 105 us
  matrix products  31.5 us (30%)
  blocking collectives  18.6 us (18%)
  waiting for transfers between devices  17.7 us (17%)
  starting transfers between devices  15.4 us (15%)
  other arithmetic  12.6 us (12%)
  local copies, waits for them, and re-layouts  8.11 us (8%)
  loops' own time  1.34 us (1%)
    all_to_all x1, blocking collectives, device_step(): mixed_local = lax.all_to_all(mixed, 'sp', 0, 1, tiled=True)  18.6 us
    all_to_all x1, waiting for transfers between devices, device_step(): q_heads = lax.all_to_all(q_local, 'sp', 1, 0, tiled=True)  12.6 us
    dot_general x1, matrix products, finish(): jnp.dot(mixed.reshape(tokens, -1), w_o, preferred_element_type=jnp.float32)  9.39 us
    dot_general x1, matrix products, project(): jnp.dot(normed, w_q, preferred_element_type=jnp.float32)  8.22 us
    dot_general x2, matrix products, one_block(): jnp.einsum('kgqs,skd->qkgd', attn_prob, v_all, preferred_element_type=jnp...  6.92 us
    all_to_all x1, starting transfers between devices, device_step(): lax.all_to_all(jnp.repeat(k_local, copies, axis=1), 'sp', 1, 0, tiled=True)  6.01 us
    all_to_all x1, waiting for transfers between devices, device_step(): lax.all_to_all(jnp.repeat(v_local, copies, axis=1), 'sp', 1, 0, tiled=True)  5.05 us
    reduce_sum x2, other arithmetic, one_block(): attn_prob = jax.nn.softmax(scores, axis=-1).astype(jnp.bfloat16)  4.87 us
  transfers between devices with their start and end apart: 3, of which 2 were waited for; matrix products, arithmetic and copies ran while one was open for 15% of the time, Pallas kernels for 0%

commit v1 on v0

v1 whole, which is shorter than its diff:
```python
import functools
import numpy as np
import jax
import jax.numpy as jnp
from jax import lax
from jax.experimental import pallas as pl
from jax.experimental.pallas import tpu as pltpu
from jax.sharding import PartitionSpec as P

EPS = 1e-6
THETA = 1000000.0
LOG2E = 1.4426950408889634
MESH = pl.DeviceIdType.MESH
CORES = 2
CHIPS = 4
BF16 = jnp.bfloat16
F32 = jnp.float32


def rope_tables(rows, head_dim):
    half = head_dim // 2
    inv_freq = np.power(np.float32(THETA), -(np.arange(half, dtype=np.float32) * np.float32(2.0 / head_dim)))
    angles = np.arange(rows, dtype=np.float32)[:, None] * inv_freq.astype(np.float32)[None, :]
    cos = np.cos(angles.astype(np.float64)).astype(np.float32)
    sin = np.sin(angles.astype(np.float64)).astype(np.float32)
    return np.concatenate([cos, cos], axis=1), np.concatenate([-sin, sin], axis=1)


def kernel(x_hbm, ln_hbm, wq_hbm, wk_hbm, wv_hbm, wo_hbm, qg_hbm, kg_hbm, cos_hbm, sin_hbm, out_hbm,
           x_v, ln_v, qg_v, kg_v, cos_v, sin_v, wkv_v, wq_v, wo_v, h_v, pk_v, kv_v, q_v, acc_v, m_v, l_v,
           o_v, os_v, y_v, out_v,
           ld_sem, wkv_sem, wq_sem, wo_sem, out_sem, h_sem, kvp_sem, kvu_sem, kvd_sem, rel_sem, kv_sem, o_sem):
    rows, feats = x_v.shape[1], x_v.shape[2]
    head = cos_v.shape[-1]
    pair = CORES * rows
    halves = wkv_v.shape[0]
    group = q_v.shape[0] // halves
    width = group * head
    scale = head ** -0.5 * LOG2E
    qcols = wq_v.shape[2]
    qparts = width // qcols
    ocols = 512

    dp = lax.axis_index("dp")
    sp = lax.axis_index("sp")
    c = lax.div(sp, CORES)
    s = lax.rem(sp, CORES)
    mate = c * CORES + (1 - s)
    up = lax.rem(c + 1, CHIPS)
    down = lax.rem(c + CHIPS - 1, CHIPS)
    first, last = c == 0, c == CHIPS - 1
    mine = c * CORES + s

    def dev(chip, core):
        return (dp, chip * CORES + core)

    loads = [
        pltpu.make_async_copy(x_hbm, x_v.at[0], ld_sem.at[0]),
        pltpu.make_async_copy(ln_hbm, ln_v, ld_sem.at[1]),
        pltpu.make_async_copy(qg_hbm, qg_v, ld_sem.at[2]),
        pltpu.make_async_copy(kg_hbm, kg_v, ld_sem.at[3]),
        pltpu.make_async_copy(cos_hbm.at[pl.ds(pl.multiple_of(c * pair, pair), pair)], cos_v, ld_sem.at[4]),
        pltpu.make_async_copy(sin_hbm.at[pl.ds(pl.multiple_of(c * pair, pair), pair)], sin_v, ld_sem.at[5]),
    ]
    kvw = CORES * head

    def wkv_load(j, which):
        src = (wk_hbm, wv_hbm)[which]
        return pltpu.make_async_copy(src.at[:, pl.ds(j * kvw, kvw)], wkv_v.at[j, :, pl.ds(which * kvw, kvw)], wkv_sem.at[j, which])

    def wq_load(i):
        j, part = divmod(i, qparts)
        col = (CORES * j + s) * width + part * qcols
        return pltpu.make_async_copy(wq_hbm.at[:, pl.ds(pl.multiple_of(col, qcols), qcols)], wq_v.at[i], wq_sem.at[i])

    def wo_load(i):
        return pltpu.make_async_copy(wo_hbm.at[pl.ds(i * width, width)], wo_v.at[i], wo_sem.at[i])

    n_wq = halves * qparts
    n_wo = CORES * halves
    loads[0].start()
    loads[1].start()
    for j in range(halves):
        wkv_load(j, 0).start()
        wkv_load(j, 1).start()
        if j == 0:
            for load in loads[2:]:
                load.start()
    for i in range(n_wq):
        wq_load(i).start()

    barrier = pltpu.get_barrier_semaphore()
    pl.semaphore_signal(barrier, inc=1, device_id=(dp, mate), device_id_type=MESH)
    for chip in (up, down):
        for core in range(CORES):
            pl.semaphore_signal(barrier, inc=1, device_id=dev(chip, core), device_id_type=MESH)

    def remote(src, dst, send, recv, to):
        return pltpu.make_async_remote_copy(src_ref=src, dst_ref=dst, send_sem=send, recv_sem=recv, device_id=to, device_id_type=MESH)

    h_copy = remote(h_v.at[s], h_v.at[s], h_sem.at[0], h_sem.at[1], (dp, mate))

    def to_mate(j):
        return remote(pk_v.at[j, 1 - s], kv_v.at[j, mine], kvp_sem.at[j], kv_sem.at[j, mine], (dp, mate))

    def to_up(j, core):
        return remote(pk_v.at[j, core], kv_v.at[j, mine], kvu_sem.at[j, core], kv_sem.at[j, mine], dev(up, core))

    def to_down(j, core):
        return remote(pk_v.at[j, core], kv_v.at[j, mine], kvd_sem.at[j, core], kv_sem.at[j, mine], dev(down, core))

    def relay(j, block, slot, chip):
        return remote(kv_v.at[j, block], kv_v.at[j, block], rel_sem.at[j, slot], kv_sem.at[j, block], dev(chip, s))

    def kv_wait(j, block):
        remote(kv_v.at[j, block], kv_v.at[j, block], kvp_sem.at[0], kv_sem.at[j, block], (dp, mate)).wait_recv()

    def o_copy(j):
        return remote(os_v.at[j], o_v.at[CORES * j + s], o_sem.at[0, j], o_sem.at[1, CORES * j + s], (dp, mate))

    sends_down = jnp.logical_or(first, jnp.logical_and(c == 1, s == 1))

    loads[0].wait()
    loads[1].wait()
    gain = ln_v[...].astype(F32).reshape(1, feats)
    step = 32

    def norm_rows(r, _):
        x = x_v[0, pl.ds(pl.multiple_of(r * step, step), step), :].astype(F32)
        inv = lax.rsqrt(jnp.mean(x * x, axis=-1, keepdims=True) + EPS)
        h_v[s, pl.ds(pl.multiple_of(r * step, step), step), :] = (x * inv * gain).astype(BF16)
        return 0

    lax.fori_loop(0, rows // step, norm_rows, 0)
    pl.semaphore_wait(barrier, 1 + 2 * CORES)
    h_copy.start()
    for load in loads[2:]:
        load.wait()
    q_gain = qg_v[...].astype(F32).reshape(1, head)
    k_gain = kg_v[...].astype(F32).reshape(1, head)

    def norm_rope(t, g, cos, sin):
        t = t * lax.rsqrt(jnp.mean(t * t, axis=-1, keepdims=True) + EPS) * g
        return (t * cos + pltpu.roll(t, head // 2, 1) * sin).astype(BF16)

    for j in range(halves):
        wkv_load(j, 0).wait()
        wkv_load(j, 1).wait()
        raw = jnp.dot(h_v[s], wkv_v[j], preferred_element_type=F32)
        own = pl.ds(pl.multiple_of(s * rows, rows), rows)
        cos, sin = cos_v[own, :], sin_v[own, :]
        for core in range(CORES):
            pk_v[j, core, 0] = norm_rope(raw[:, core * head:(core + 1) * head], k_gain, cos, sin)
            pk_v[j, core, 1] = raw[:, kvw + core * head:kvw + (core + 1) * head].astype(BF16)
        for core in range(CORES):
            @pl.when(jnp.logical_not(last))
            def _():
                to_up(j, core).start()

            @pl.when(sends_down)
            def _():
                to_down(j, core).start()
        to_mate(j).start()
        kv_v[j, mine] = pk_v[j, s]

    h_copy.wait_recv()

    def project_q(i, _):
        pltpu.make_async_copy(wq_hbm.at[:, pl.ds(0, qcols)], wq_v.at[i], wq_sem.at[i]).wait()
        raw = jnp.dot(h_v[...].reshape(pair, feats), wq_v[i], preferred_element_type=F32)
        for g in range(qcols // head):
            q_v[i * (qcols // head) + g] = norm_rope(raw[:, g * head:(g + 1) * head], q_gain, cos_v[...], sin_v[...])
        return 0

    for i in range(n_wo):
        wo_load(i).start()
    lax.fori_loop(0, n_wq, project_q, 0)

    @pl.when(first)
    def _():
        for j in range(halves):
            kv_wait(j, 2 * CORES - 1)
            relay(j, 2 * CORES - 1, 0, down).start()

    def attend(j, block, diagonal):
        keys = kv_v[j, pl.ds(block * CORES, CORES), 0].reshape(pair, head)
        vals = kv_v[j, pl.ds(block * CORES, CORES), 1].reshape(pair, head)
        if diagonal:
            row = lax.broadcasted_iota(jnp.int32, (pair, pair), 0)
            col = lax.broadcasted_iota(jnp.int32, (pair, pair), 1)
            seen = row >= col
        for g in range(group):
            i = j * group + g
            sc = lax.dot_general(q_v[i], keys, (((1,), (1,)), ((), ())), preferred_element_type=F32)
            if diagonal:
                sc = jnp.where(seen, sc, -jnp.inf)
            top = jnp.max(sc, axis=-1, keepdims=True) * scale
            if diagonal:
                new = jnp.broadcast_to(top, (pair, head))
            else:
                old = m_v[i]
                new = jnp.maximum(old, top)
            m_v[i] = new
            probs = [jnp.exp2(sc[:, k * head:(k + 1) * head] * scale - new) for k in range(pair // head)]
            total = sum(probs[1:], probs[0])
            mixed = jnp.dot(jnp.concatenate(probs, axis=1).astype(BF16), vals, preferred_element_type=F32)
            if diagonal:
                l_v[i] = total
                acc_v[i] = mixed
            else:
                fade = jnp.exp2(old - new)
                l_v[i] = l_v[i] * fade + total
                acc_v[i] = acc_v[i] * fade + mixed

    def project_out(i, final):
        for n in range(feats // ocols):
            cols = slice(n * ocols, (n + 1) * ocols)
            part = jnp.dot(o_v[i], wo_v[i, :, cols], preferred_element_type=F32)
            y_v[:, cols] += part

    y_v[...] = x_v[0].astype(F32)

    def one_step(idx, _):
        t = lax.div(idx, halves)
        j = lax.rem(idx, halves)

        @pl.when(t == 0)
        def _():
            kv_wait(j, mate)
            attend(j, c, True)

        @pl.when(t > 0)
        def _():
            block = c - t + lax.div(c, CHIPS - 1) * lax.div(t, 2) * (2 * lax.rem(t, 2) - 1)

            @pl.when(jnp.logical_or(jnp.logical_not(last), t != 2))
            def _():
                for core in range(CORES):
                    kv_wait(j, block * CORES + core)

            @pl.when(jnp.logical_and(c == 2, t == 1))
            def _():
                relay(j, CORES, 0, up).start()

            @pl.when(jnp.logical_and(last, t == 1))
            def _():
                for core in range(CORES):
                    kv_wait(j, core)
                    relay(j, core, core, down).start()

            attend(j, block, False)

        @pl.when(t == c)
        def _():
            for g in range(group):
                i = j * group + g
                inv = 1.0 / jnp.sum(l_v[i], axis=-1, keepdims=True)
                o = (acc_v[i] * inv).astype(BF16)
                acc_v[i] = acc_v[i] * inv
            for g in range(group):
                i = j * group + g
                theirs = pl.ds(pl.multiple_of((1 - s) * rows, rows), rows)
                ours = pl.ds(pl.multiple_of(s * rows, rows), rows)
                os_v[j, :, g * head:(g + 1) * head] = acc_v[i, theirs, :].astype(BF16)
                o_v[CORES * j + s, :, g * head:(g + 1) * head] = acc_v[i, ours, :].astype(BF16)
            o_copy(j).start()
            i = CORES * j + s
            pltpu.make_async_copy(wo_hbm.at[pl.ds(0, width)], wo_v.at[i], wo_sem.at[i]).wait()
            project_out(i, False)

        return 0

    lax.fori_loop(0, halves * (c + 1), one_step, 0)

    def theirs_out(j, _):
        i = CORES * j + 1 - s
        remote(os_v.at[j], o_v.at[i], o_sem.at[0, j], o_sem.at[1, i], (dp, mate)).wait_recv()
        pltpu.make_async_copy(wo_hbm.at[pl.ds(0, width)], wo_v.at[i], wo_sem.at[i]).wait()
        project_out(i, False)
        return 0

    lax.fori_loop(0, halves, theirs_out, 0)
    out_v[...] = y_v[...].astype(BF16)
    out = pltpu.make_async_copy(out_v, out_hbm, out_sem)
    out.start()

    h_copy.wait_send()
    for j in range(halves):
        to_mate(j).wait_send()
        o_copy(j).wait_send()
        for core in range(CORES):
            @pl.when(jnp.logical_not(last))
            def _():
                to_up(j, core).wait_send()

            @pl.when(sends_down)
            def _():
                to_down(j, core).wait_send()

            @pl.when(last)
            def _():
                relay(j, core, core, down).wait_send()

        @pl.when(first)
        def _():
            relay(j, 2 * CORES - 1, 0, down).wait_send()

        @pl.when(c == 2)
        def _():
            relay(j, CORES, 0, up).wait_send()
    out.wait()


def solution(mesh):
    group_size = mesh.shape['sp']
    assert group_size == CORES * CHIPS

    def device_step(hidden, ln_gain, w_q, w_k, w_v, w_o, q_gain, k_gain):
        rows, feats = hidden.shape
        head = q_gain.shape[0]
        kv_heads = w_k.shape[1] // head
        q_heads = w_q.shape[1] // head
        halves = kv_heads // CORES
        group = q_heads // kv_heads
        width = group * head
        pair = CORES * rows
        qcols = 512
        n_wq = halves * width // qcols
        cos, sin = rope_tables(group_size * rows, head)
        dma = pltpu.SemaphoreType.DMA
        any_spec = pl.BlockSpec(memory_space=pl.ANY)
        scratch = [
            pltpu.VMEM((1, rows, feats), BF16),
            pltpu.VMEM((1, feats), BF16),
            pltpu.VMEM((1, head), BF16),
            pltpu.VMEM((1, head), BF16),
            pltpu.VMEM((pair, head), F32),
            pltpu.VMEM((pair, head), F32),
            pltpu.VMEM((halves, feats, 2 * CORES * head), BF16),
            pltpu.VMEM((n_wq, feats, qcols), BF16),
            pltpu.VMEM((kv_heads, width, feats), BF16),
            pltpu.VMEM((CORES, rows, feats), BF16),
            pltpu.VMEM((halves, CORES, 2, rows, head), BF16),
            pltpu.VMEM((halves, group_size, 2, rows, head), BF16),
            pltpu.VMEM((halves * group, pair, head), BF16),
            pltpu.VMEM((halves * group, pair, head), F32),
            pltpu.VMEM((halves * group, pair, head), F32),
            pltpu.VMEM((halves * group, pair, head), F32),
            pltpu.VMEM((kv_heads, rows, width), BF16),
            pltpu.VMEM((halves, rows, width), BF16),
            pltpu.VMEM((rows, feats), F32),
            pltpu.VMEM((rows, feats), BF16),
            dma((6,)), dma((halves, 2)), dma((n_wq,)), dma((kv_heads,)), dma, dma((2,)),
            dma((halves,)), dma((halves, CORES)), dma((halves, CORES)), dma((halves, CORES)),
            dma((halves, group_size)), dma((2, kv_heads)),
        ]
        return pl.pallas_call(
            kernel,
            out_shape=jax.ShapeDtypeStruct((rows, feats), BF16),
            in_specs=[any_spec] * 10,
            out_specs=any_spec,
            scratch_shapes=scratch,
            compiler_params=pltpu.CompilerParams(
                collective_id=0, has_side_effects=True, vmem_limit_bytes=60 * 2 ** 20
            ),
            name="attention_block",
        )(hidden, ln_gain.reshape(1, -1), w_q, w_k, w_v, w_o, q_gain.reshape(1, -1), k_gain.reshape(1, -1),
          jnp.asarray(cos), jnp.asarray(sin))

    row_spec = P(('dp', 'sp'), None)
    return jax.shard_map(device_step, mesh=mesh, in_specs=(row_spec, P(), P(), P(), P(), P(), P(), P()), out_specs=row_spec, check_vma=False)
```

time: 106 us -> 28.6 us (0.27)
  the two profiles are of different devices: /device:TPU:81 before, /device:TPU:125 now
where the time goes in v1:
time: 28.6 us; the launch traced here: 28.4 us
  Pallas kernels  25.2 us (88%)
  local copies, waits for them, and re-layouts  3.17 us (11%)
    pallas_call x1, Pallas kernels, device_step(): pl.pallas_call(kernel, out_shape=jax.ShapeDtypeStruct((rows, feats), BF16...  25.2 us
    unnamed x1, local copies, waits for them, and re-layouts  1.88 us
    reshape x1, local copies, waits for them, and re-layouts, device_step(): ln_gain.reshape(1, -1)  1.29 us

profile of v1, /device:TPU:125, one launch (start us, length us, event | category | flops | bytes accessed | tf_op | source)
XLA Modules:
  0.0 28.4 jit_solution(6546839006518147027)
XLA Ops:
  0.0 1.3 %reshape.9.ln_hbm = bf16[1,2048]{1,0:T(2,128)(2,1)} reshape(bf16[2048]{0:T(1024)(128)(2,1)} %param.11) | data formatting | bytes 8192 | tf_op jit(solution)/shard_map/reshape | solution.py:367
  1.3 25.2 %attention_block.1 = bf16[128,2048]{1,0:T(8,128)(2,1)} custom-call(bf16[128,2048]{1,0:T(8,128)(2,1)} %x_hbm.1, bf16[1,2048]{1,0:T(2,128)(2,1)} %reshape.9.ln_hbm, bf16[2048,4096]{1,0:T(8,128)(2,1)} %wq_hbm.1, bf16[2048,512]{1,0:T(8,128)(2,1)} %wk_hbm.1, bf16[2048,512]{1,0:T(8,128)(2,1)} %wv_hbm.1, bf16[4096,2048]{1,0:T(8,128)(2,1)} %wo_hbm.1, ...), custom_call_target="tpu_custom_call" | custom-call | tf_op jit(solution)/shard_map/attention_block/pallas_call | solution.py:357
  26.5 1.9 %copy.12 = bf16[128,2048]{1,0:T(8,128)(2,1)} copy(bf16[128,2048]{1,0:T(8,128)(2,1)} %attention_block.1) | data formatting | bytes 1048576

commit v2 on v1

v2 whole, which is shorter than its diff:
```python
import functools
import numpy as np
import jax
import jax.numpy as jnp
from jax import lax
from jax.experimental import pallas as pl
from jax.experimental.pallas import tpu as pltpu
from jax.sharding import PartitionSpec as P

EPS = 1e-6
THETA = 1000000.0
LOG2E = 1.4426950408889634
MESH = pl.DeviceIdType.MESH
CORES = 2
CHIPS = 4
BF16 = jnp.bfloat16
F32 = jnp.float32


def rope_tables(rows, head_dim):
    half = head_dim // 2
    inv_freq = np.power(np.float32(THETA), -(np.arange(half, dtype=np.float32) * np.float32(2.0 / head_dim)))
    angles = np.arange(rows, dtype=np.float32)[:, None] * inv_freq.astype(np.float32)[None, :]
    cos = np.cos(angles.astype(np.float64)).astype(np.float32)
    sin = np.sin(angles.astype(np.float64)).astype(np.float32)
    return np.concatenate([cos, cos], axis=1), np.concatenate([-sin, sin], axis=1)


def kernel(x_hbm, ln_hbm, wq_hbm, wk_hbm, wv_hbm, wo_hbm, qg_hbm, kg_hbm, rope_hbm, ropet_hbm, y_v,
           x_v, ln_v, qg_v, kg_v, rope_v, ropet_v, wkv_v, wq_v, wo_v, h_v, pk_v, kv_v, raw_v, q_v, s_v, acc_v, m_v, l_v,
           oo_v, or_v,
           ld_sem, wkv_sem, wq_sem, wo_sem, h_sem, kvp_sem, kvu_sem, kvd_sem, rel_sem, kv_sem, o_sem):
    rows, feats = x_v.shape[1], x_v.shape[2]
    head = rope_v.shape[-1]
    pair = CORES * rows
    halves = wkv_v.shape[0]
    group = q_v.shape[0] // halves
    width = group * head
    scale = head ** -0.5 * LOG2E
    qcols = wq_v.shape[2]
    qparts = width // qcols
    ocols = 512

    dp = lax.axis_index("dp")
    sp = lax.axis_index("sp")
    c = lax.div(sp, CORES)
    s = lax.rem(sp, CORES)
    mate = c * CORES + (1 - s)
    up = lax.rem(c + 1, CHIPS)
    down = lax.rem(c + CHIPS - 1, CHIPS)
    first, last = c == 0, c == CHIPS - 1
    mine = c * CORES + s

    def dev(chip, core):
        return (dp, chip * CORES + core)

    loads = [
        pltpu.make_async_copy(x_hbm, x_v.at[0], ld_sem.at[0]),
        pltpu.make_async_copy(ln_hbm, ln_v, ld_sem.at[1]),
        pltpu.make_async_copy(qg_hbm, qg_v, ld_sem.at[2]),
        pltpu.make_async_copy(kg_hbm, kg_v, ld_sem.at[3]),
        pltpu.make_async_copy(rope_hbm.at[c * CORES + s], rope_v, ld_sem.at[4]),
        pltpu.make_async_copy(ropet_hbm.at[c], ropet_v, ld_sem.at[5]),
    ]
    kvw = CORES * head

    def wkv_load(j, which):
        src = (wk_hbm, wv_hbm)[which]
        return pltpu.make_async_copy(src.at[:, pl.ds(j * kvw, kvw)], wkv_v.at[j, :, pl.ds(which * kvw, kvw)], wkv_sem.at[j, which])

    def wq_load(i):
        j, part = divmod(i, qparts)
        col = (CORES * j + s) * width + part * qcols
        return pltpu.make_async_copy(wq_hbm.at[:, pl.ds(pl.multiple_of(col, qcols), qcols)], wq_v.at[i], wq_sem.at[i])

    def wo_load(i):
        return pltpu.make_async_copy(wo_hbm.at[pl.ds(i * width, width)], wo_v.at[i], wo_sem.at[i])

    n_wq = halves * qparts
    n_wo = CORES * halves
    stages = [wkv_load(j, which) for j in range(halves) for which in range(2)]
    for load in loads[:5] + stages + loads[5:]:
        load.start()

    barrier = pltpu.get_barrier_semaphore()
    pl.semaphore_signal(barrier, inc=1, device_id=(dp, mate), device_id_type=MESH)
    for chip in (up, down):
        for core in range(CORES):
            pl.semaphore_signal(barrier, inc=1, device_id=dev(chip, core), device_id_type=MESH)

    def remote(src, dst, send, recv, to):
        return pltpu.make_async_remote_copy(src_ref=src, dst_ref=dst, send_sem=send, recv_sem=recv, device_id=to, device_id_type=MESH)

    h_copy = remote(h_v.at[s], h_v.at[s], h_sem.at[0], h_sem.at[1], (dp, mate))

    def to_mate(j):
        return remote(pk_v.at[j, 1 - s], kv_v.at[j, mine], kvp_sem.at[j], kv_sem.at[j, mine], (dp, mate))

    def to_up(j, core):
        return remote(pk_v.at[j, core], kv_v.at[j, mine], kvu_sem.at[j, core], kv_sem.at[j, mine], dev(up, core))

    def to_down(j, core):
        return remote(pk_v.at[j, core], kv_v.at[j, mine], kvd_sem.at[j, core], kv_sem.at[j, mine], dev(down, core))

    def relay(j, block, slot, chip):
        return remote(kv_v.at[j, block], kv_v.at[j, block], rel_sem.at[j, slot], kv_sem.at[j, block], dev(chip, s))

    def kv_wait(j, block):
        remote(kv_v.at[j, block], kv_v.at[j, block], kvp_sem.at[0], kv_sem.at[j, block], (dp, mate)).wait_recv()

    def o_copy(j):
        return remote(oo_v.at[j, 1 - s], or_v.at[j], o_sem.at[0, j], o_sem.at[1, j], (dp, mate))

    sends_down = jnp.logical_or(first, jnp.logical_and(c == 1, s == 1))

    loads[0].wait()
    loads[1].wait()
    gain = jnp.concatenate([ln_v[k:k + 1, :] for k in range(feats // head)], axis=1).astype(F32)
    step = 64

    def norm_rows(r, _):
        x = x_v[0, pl.ds(pl.multiple_of(r * step, step), step), :].astype(F32)
        inv = lax.rsqrt(jnp.mean(x * x, axis=-1, keepdims=True) + EPS)
        h_v[s, pl.ds(pl.multiple_of(r * step, step), step), :] = (x * inv * gain).astype(BF16)
        return 0

    lax.fori_loop(0, rows // step, norm_rows, 0)
    pl.semaphore_wait(barrier, 1 + 2 * CORES)
    h_copy.start()
    for load in loads[2:5]:
        load.wait()
    k_gain = kg_v[...].astype(F32).reshape(1, head)

    def norm_rope(t, g, cos, sin):
        t = t * lax.rsqrt(jnp.mean(t * t, axis=-1, keepdims=True) + EPS) * g
        return (t * cos + pltpu.roll(t, head // 2, 1) * sin).astype(BF16)

    def finish_kv(j):
        for core in range(CORES):
            pk_v[j, core, 0] = norm_rope(raw_v[j, :rows, core * head:(core + 1) * head], k_gain, rope_v[0], rope_v[1])
            pk_v[j, core, 1] = raw_v[j, :rows, kvw + core * head:kvw + (core + 1) * head].T.astype(BF16)

    def send_kv(j):
        for core in range(CORES):
            @pl.when(jnp.logical_not(last))
            def _():
                to_up(j, core).start()

            @pl.when(sends_down)
            def _():
                to_down(j, core).start()
        to_mate(j).start()
        kv_v[j, mine] = pk_v[j, s]

    for j in range(halves):
        wkv_load(j, 0).wait()
        wkv_load(j, 1).wait()
        for i in range(qparts):
            wq_load(qparts * j + i).start()
        raw_v[j, :rows] = jnp.dot(h_v[s], wkv_v[j], preferred_element_type=F32)
        if j:
            finish_kv(j - 1)
        if j:
            send_kv(j - 1)
    finish_kv(halves - 1)
    send_kv(halves - 1)

    h_copy.wait_recv()

    loads[5].wait()
    q_gain = jnp.broadcast_to(qg_v[...].astype(F32), (head, head)).T
    q_gain = jnp.concatenate([q_gain] * CORES, axis=1)

    def turn(t):
        return jnp.concatenate([t[head // 2:], t[:head // 2]], axis=0)

    ropet_v[0] = ropet_v[0] * q_gain
    ropet_v[1] = ropet_v[1] * turn(q_gain)

    def finish_q(i):
        for g in range(qcols // head):
            t = raw_v[i % 2, :, g * head:(g + 1) * head].T
            t = t * lax.rsqrt(jnp.mean(t * t, axis=0, keepdims=True) + EPS)
            q_v[i * (qcols // head) + g] = (t * ropet_v[0] + turn(t) * ropet_v[1]).astype(BF16)

    for i in range(n_wq):
        wq_load(i).wait()
        wo_load(i).start()
        raw_v[i % 2] = jnp.dot(h_v[...].reshape(pair, feats), wq_v[i], preferred_element_type=F32)
        if i:
            finish_q(i - 1)
    finish_q(n_wq - 1)

    @pl.when(first)
    def _():
        for j in range(halves):
            kv_wait(j, 2 * CORES - 1)
            relay(j, 2 * CORES - 1, 0, down).start()

    def relay_first(j):
        for core in range(CORES):
            kv_wait(j, core)
            relay(j, core, core, down).start()

    @pl.when(last)
    def _():
        relay_first(0)

    def attend(j, block, diagonal):
        keys = kv_v[j, pl.ds(block * CORES, CORES), 0].reshape(pair, head)
        vals = jnp.concatenate([kv_v[j, block * CORES + core, 1] for core in range(CORES)], axis=1)
        if diagonal:
            key = lax.broadcasted_iota(jnp.int32, (pair, pair), 0)
            row = lax.broadcasted_iota(jnp.int32, (pair, pair), 1)
            seen = key <= row

        def score(g):
            i = j * group + g
            sc = jnp.dot(keys, q_v[i], preferred_element_type=F32)
            if diagonal:
                sc = jnp.where(seen, sc, -jnp.inf)
            s_v[i] = sc
            return jnp.max(sc, axis=0, keepdims=True) * scale

        def mix(g, new):
            i = j * group + g
            if not diagonal:
                old = m_v[i]
                new = jnp.maximum(old, new)
            m_v[i] = new
            probs = jnp.exp2(s_v[i] * scale - new)
            total = jnp.sum(probs, axis=0, keepdims=True)
            mixed = jnp.dot(vals, probs.astype(BF16), preferred_element_type=F32)
            if diagonal:
                l_v[i] = total
                acc_v[i] = mixed
            else:
                fade = jnp.exp2(old - new)
                l_v[i] = l_v[i] * fade + total
                acc_v[i] = acc_v[i] * fade + mixed

        tops = [score(g) for g in range(group)]
        for g in range(group):
            mix(g, tops[g])

    def project_out(o_ref, i):
        for n in range(feats // ocols):
            cols = slice(n * ocols, (n + 1) * ocols)
            y_v[:, cols] += jnp.dot(o_ref[...], wo_v[i, :, cols], preferred_element_type=F32)

    y_v[...] = jnp.zeros_like(y_v)

    def one_step(idx, _):
        swap = lax.div(c, CHIPS - 1) * lax.rem(lax.div(idx + 2, 4), 2)
        t = (1 - swap) * lax.div(idx, 2) + swap * (1 + lax.rem(idx, 2))
        j = (1 - swap) * lax.rem(idx, 2) + swap * (lax.div(idx, 2) - 1)

        @pl.when(t == 0)
        def _():
            kv_wait(j, mate)
            attend(j, c, True)

        @pl.when(t > 0)
        def _():
            block = c - t + lax.div(c, CHIPS - 1) * lax.div(t, 2) * (2 * lax.rem(t, 2) - 1)

            @pl.when(jnp.logical_or(jnp.logical_not(last), t != 2))
            def _():
                for core in range(CORES):
                    kv_wait(j, block * CORES + core)

            @pl.when(jnp.logical_and(c == 2, t == 1))
            def _():
                relay(j, CORES, 0, up).start()

            @pl.when(jnp.logical_and(last, idx == halves + 1))
            def _():
                relay_first(1)

            attend(j, block, False)

        @pl.when(t == c)
        def _():
            for g in range(group):
                i = j * group + g
                o = acc_v[i] * (1.0 / l_v[i])
                for core in range(CORES):
                    oo_v[j, core, :, g * head:(g + 1) * head] = o[:, core * rows:(core + 1) * rows].T.astype(BF16)
            o_copy(j).start()
            i = CORES * j + s
            pltpu.make_async_copy(wo_hbm.at[pl.ds(0, width)], wo_v.at[i], wo_sem.at[i]).wait()
            project_out(oo_v.at[j, s], i)

        return 0

    lax.fori_loop(0, halves * (c + 1), one_step, 0)

    def theirs_out(j, _):
        i = CORES * j + 1 - s
        o_copy(j).wait_recv()
        pltpu.make_async_copy(wo_hbm.at[pl.ds(0, width)], wo_v.at[i], wo_sem.at[i]).wait()
        project_out(or_v.at[j], i)
        return 0

    lax.fori_loop(0, halves, theirs_out, 0)

    h_copy.wait_send()
    for j in range(halves):
        to_mate(j).wait_send()
        o_copy(j).wait_send()
        for core in range(CORES):
            @pl.when(jnp.logical_not(last))
            def _():
                to_up(j, core).wait_send()

            @pl.when(sends_down)
            def _():
                to_down(j, core).wait_send()

            @pl.when(last)
            def _():
                relay(j, core, core, down).wait_send()

        @pl.when(first)
        def _():
            relay(j, 2 * CORES - 1, 0, down).wait_send()

        @pl.when(c == 2)
        def _():
            relay(j, CORES, 0, up).wait_send()


def solution(mesh):
    group_size = mesh.shape['sp']
    assert group_size == CORES * CHIPS

    def device_step(hidden, ln_gain, w_q, w_k, w_v, w_o, q_gain, k_gain):
        rows, feats = hidden.shape
        head = q_gain.shape[0]
        kv_heads = w_k.shape[1] // head
        q_heads = w_q.shape[1] // head
        halves = kv_heads // CORES
        group = q_heads // kv_heads
        width = group * head
        pair = CORES * rows
        qcols = 512
        n_wq = halves * width // qcols
        tables = np.stack(rope_tables(group_size * rows, head))
        by_device = tables.reshape(2, group_size, rows, head).transpose(1, 0, 2, 3)
        by_chip = tables.reshape(2, CHIPS, pair, head).transpose(1, 0, 3, 2)
        dma = pltpu.SemaphoreType.DMA
        any_spec = pl.BlockSpec(memory_space=pl.ANY)
        scratch = [
            pltpu.VMEM((1, rows, feats), BF16),
            pltpu.VMEM((feats // head, head), BF16),
            pltpu.VMEM((1, head), BF16),
            pltpu.VMEM((1, head), BF16),
            pltpu.VMEM((2, rows, head), F32),
            pltpu.VMEM((2, head, pair), F32),
            pltpu.VMEM((halves, feats, 2 * CORES * head), BF16),
            pltpu.VMEM((n_wq, feats, qcols), BF16),
            pltpu.VMEM((kv_heads, width, feats), BF16),
            pltpu.VMEM((CORES, rows, feats), BF16),
            pltpu.VMEM((halves, CORES, 2, rows, head), BF16),
            pltpu.VMEM((halves, group_size, 2, rows, head), BF16),
            pltpu.VMEM((2, pair, qcols), F32),
            pltpu.VMEM((halves * group, head, pair), BF16),
            pltpu.VMEM((halves * group, pair, pair), F32),
            pltpu.VMEM((halves * group, head, pair), F32),
            pltpu.VMEM((halves * group, 1, pair), F32),
            pltpu.VMEM((halves * group, 1, pair), F32),
            pltpu.VMEM((halves, CORES, rows, width), BF16),
            pltpu.VMEM((halves, rows, width), BF16),
            dma((6,)), dma((halves, 2)), dma((n_wq,)), dma((kv_heads,)), dma((2,)),
            dma((halves,)), dma((halves, CORES)), dma((halves, CORES)), dma((halves, CORES)),
            dma((halves, group_size)), dma((2, halves)),
        ]
        mixed = pl.pallas_call(
            kernel,
            out_shape=pltpu.VMEM((rows, feats), F32),
            in_specs=[any_spec] * 10,
            out_specs=pl.BlockSpec(memory_space=pltpu.VMEM),
            scratch_shapes=scratch,
            compiler_params=pltpu.CompilerParams(
                collective_id=0, has_side_effects=True, vmem_limit_bytes=56 * 2 ** 20
            ),
            name="attention_block",
        )(hidden, ln_gain.reshape(-1, head), w_q, w_k, w_v, w_o, q_gain.reshape(1, -1), k_gain.reshape(1, -1),
          jnp.asarray(by_device), jnp.asarray(by_chip))
        return (hidden.astype(F32) + mixed).astype(BF16)

    row_spec = P(('dp', 'sp'), None)
    return jax.shard_map(device_step, mesh=mesh, in_specs=(row_spec, P(), P(), P(), P(), P(), P(), P()), out_specs=row_spec, check_vma=False)
```

time: 28.6 us -> 21.2 us (0.74)
  the two profiles are of different devices: /device:TPU:125 before, /device:TPU:87 now
where the time goes in v2:
time: 21.2 us; the launch traced here: 21.1 us
  Pallas kernels  20.2 us (95%)
  other arithmetic  0.9 us (4%)
    pallas_call x1, Pallas kernels, device_step(): pl.pallas_call(kernel, out_shape=pltpu.VMEM((rows, feats), F32), in_specs...  20.2 us
    convert_element_type x1, other arithmetic, device_step(): return (hidden.astype(F32) + mixed).astype(BF16)  0.9 us

profile of v2, /device:TPU:87, one launch (start us, length us, event | category | flops | bytes accessed | tf_op | source)
XLA Modules:
  0.0 21.1 jit_solution(13107409618778275868)
XLA Ops:
  0.0 0.0 copy-start
  0.0 20.2 %attention_block.1 = f32[128,2048]{1,0:T(8,128)S(1)} custom-call(bf16[128,2048]{1,0:T(8,128)(2,1)} %x_hbm.1, bf16[16,128]{1,0:T(8,128)(2,1)} %bitcast.3, bf16[2048,4096]{1,0:T(8,128)(2,1)} %wq_hbm.1, bf16[2048,512]{1,0:T(8,128)(2,1)} %wk_hbm.1, bf16[2048,512]{1,0:T(8,128)(2,1)} %wv_hbm.1, bf16[4096,2048]{1,0:T(8,128)(2,1)} %wo_hbm.1, ...), custom_call_target="tpu_custom_call" | custom-call | tf_op jit(solution)/shard_map/attention_block/pallas_call | solution.py:378
  20.2 0.0 copy-done
  20.2 0.9 %add_convert_fusion = bf16[128,2048]{1,0:T(8,128)(2,1)} fusion(f32[128,2048]{1,0:T(8,128)S(1)} %attention_block.1, bf16[128,2048]{1,0:T(8,128)(2,1)S(1)} %copy-done), kind=kLoop, calls=%fused_computation | loop fusion | flops 786432 | bytes 2097152 | tf_op jit(solution)/shard_map/convert_element_type | solution.py:390
Async XLA Ops:
  0.0 20.2 %copy-start = (bf16[128,2048]{1,0:T(8,128)(2,1)S(1)}, bf16[128,2048]{1,0:T(8,128)(2,1)}, u32[]{:S(2)}) copy-start(bf16[128,2048]{1,0:T(8,128)(2,1)} %x_hbm.1) | copy-start | bytes 1572868

commit v3 on v2

--- a/solution.py
+++ b/solution.py
@@ -79,7 +79,7 @@
     n_wq = halves * qparts
     n_wo = CORES * halves
     stages = [wkv_load(j, which) for j in range(halves) for which in range(2)]
-    for load in loads[:5] + stages + loads[5:]:
+    for load in loads[:5] + stages:
         load.start()
 
     barrier = pltpu.get_barrier_semaphore()
@@ -112,9 +112,26 @@
         return remote(oo_v.at[j, 1 - s], or_v.at[j], o_sem.at[0, j], o_sem.at[1, j], (dp, mate))
 
     sends_down = jnp.logical_or(first, jnp.logical_and(c == 1, s == 1))
+    second = c == 1
+    even, odd = s == 0, s == 1
+    third = c == 2
+
+    def both(a, b):
+        return jnp.logical_and(a, b)
+
+    routes = ((0, 3, down), (1, 0, up), (2, 2, up), (3, 1, down))
+
+    def relay_now(j, chips):
+        for chip, block, to in routes[chips]:
+            @pl.when(c == chip)
+            def _():
+                kv_wait(j, block)
+                relay(j, block, 0, to).start()
 
     loads[0].wait()
     loads[1].wait()
+    loads[5].start()
+    wq_load(0).start()
     gain = jnp.concatenate([ln_v[k:k + 1, :] for k in range(feats // head)], axis=1).astype(F32)
     step = 64
 
@@ -140,30 +157,49 @@
             pk_v[j, core, 0] = norm_rope(raw_v[j, :rows, core * head:(core + 1) * head], k_gain, rope_v[0], rope_v[1])
             pk_v[j, core, 1] = raw_v[j, :rows, kvw + core * head:kvw + (core + 1) * head].T.astype(BF16)
 
+    def send_up(j):
+        for core in range(CORES):
+            to_up(j, core).start()
+
+    def send_down(j):
+        for core in range(CORES):
+            to_down(j, core).start()
+
+    def send(when, *calls):
+        @pl.when(when)
+        def _():
+            for call, j in calls:
+                call(j)
+
     def send_kv(j):
-        for core in range(CORES):
-            @pl.when(jnp.logical_not(last))
-            def _():
-                to_up(j, core).start()
-
-            @pl.when(sends_down)
-            def _():
-                to_down(j, core).start()
+        if j == 0:
+            send(jnp.logical_or(third, both(c < 2, even)), (send_up, 0))
+            send(both(c < 2, odd), (send_down, 0))
+        else:
+            send(both(first, even), (send_down, 0), (send_up, 1))
+            send(both(second, odd), (send_up, 0), (send_down, 1))
+            send(both(third, even), (send_up, 1))
         to_mate(j).start()
         kv_v[j, mine] = pk_v[j, s]
+
+    def send_rest(part):
+        if part == 0:
+            send(both(first, odd), (send_up, 0), (send_up, 1), (send_down, 1))
+            send(both(second, even), (send_up, 1))
+        else:
+            relay_now(0, slice(0, 4))
+            send(both(first, even), (send_down, 1))
+            send(jnp.logical_or(both(second, odd), both(third, odd)), (send_up, 1))
 
     for j in range(halves):
         wkv_load(j, 0).wait()
         wkv_load(j, 1).wait()
-        for i in range(qparts):
-            wq_load(qparts * j + i).start()
-        raw_v[j, :rows] = jnp.dot(h_v[s], wkv_v[j], preferred_element_type=F32)
-        if j:
-            finish_kv(j - 1)
-        if j:
-            send_kv(j - 1)
-    finish_kv(halves - 1)
-    send_kv(halves - 1)
+        raw_v[j, :rows, :2 * kvw] = jnp.dot(h_v[s], wkv_v[j], preferred_element_type=F32)
+        finish_kv(j)
+        if j == 0:
+            for i in range(1, n_wq):
+                wq_load(i).start()
+        send_kv(j)
 
     h_copy.wait_recv()
 
@@ -185,42 +221,44 @@
 
     for i in range(n_wq):
         wq_load(i).wait()
-        wo_load(i).start()
+        if i == n_wq - 1:
+            for n in range(n_wo):
+                wo_load(n).start()
         raw_v[i % 2] = jnp.dot(h_v[...].reshape(pair, feats), wq_v[i], preferred_element_type=F32)
         if i:
             finish_q(i - 1)
-    finish_q(n_wq - 1)
-
-    @pl.when(first)
-    def _():
-        for j in range(halves):
-            kv_wait(j, 2 * CORES - 1)
-            relay(j, 2 * CORES - 1, 0, down).start()
-
-    def relay_first(j):
-        for core in range(CORES):
-            kv_wait(j, core)
-            relay(j, core, core, down).start()
-
-    @pl.when(last)
-    def _():
-        relay_first(0)
-
-    def attend(j, block, diagonal):
-        keys = kv_v[j, pl.ds(block * CORES, CORES), 0].reshape(pair, head)
-        vals = jnp.concatenate([kv_v[j, block * CORES + core, 1] for core in range(CORES)], axis=1)
+        if i + 1 < n_wq:
+            send_rest(0)
+    def attend(j, blocks, diagonal):
+        keys = [kv_v[j, pl.ds(block * CORES, CORES), 0].reshape(pair, head) for block in blocks]
+        vals = jnp.concatenate([kv_v[j, block * CORES + core, 1] for block in blocks for core in range(CORES)], axis=1)
+        span = len(blocks) * pair
         if diagonal:
-            key = lax.broadcasted_iota(jnp.int32, (pair, pair), 0)
-            row = lax.broadcasted_iota(jnp.int32, (pair, pair), 1)
+            key = lax.broadcasted_iota(jnp.int32, (rows, rows), 0)
+            row = lax.broadcasted_iota(jnp.int32, (rows, rows), 1)
             seen = key <= row
+
+            def hide(sc):
+                return jnp.where(seen, sc, -jnp.inf)
 
         def score(g):
             i = j * group + g
-            sc = jnp.dot(keys, q_v[i], preferred_element_type=F32)
+            top = None
             if diagonal:
-                sc = jnp.where(seen, sc, -jnp.inf)
-            s_v[i] = sc
-            return jnp.max(sc, axis=0, keepdims=True) * scale
+                early = jnp.dot(keys[0][:rows], q_v[i], preferred_element_type=F32)
+                early = jnp.concatenate([hide(early[:, :rows]), early[:, rows:]], axis=1)
+                late = hide(jnp.dot(keys[0][rows:], q_v[i, :, rows:], preferred_element_type=F32))
+                s_v[i, :rows] = early
+                s_v[i, rows:pair, rows:] = late
+                top = jnp.max(early, axis=0, keepdims=True)
+                both = jnp.maximum(top[:, rows:], jnp.max(late, axis=0, keepdims=True))
+                return jnp.concatenate([top[:, :rows], both], axis=1) * scale
+            for n in range(len(blocks)):
+                sc = jnp.dot(keys[n], q_v[i], preferred_element_type=F32)
+                s_v[i, n * pair:(n + 1) * pair] = sc
+                best = jnp.max(sc, axis=0, keepdims=True) * scale
+                top = best if top is None else jnp.maximum(top, best)
+            return top
 
         def mix(g, new):
             i = j * group + g
@@ -228,8 +266,15 @@
                 old = m_v[i]
                 new = jnp.maximum(old, new)
             m_v[i] = new
-            probs = jnp.exp2(s_v[i] * scale - new)
-            total = jnp.sum(probs, axis=0, keepdims=True)
+            if diagonal:
+                early = jnp.exp2(s_v[i, :rows] * scale - new)
+                late = jnp.exp2(s_v[i, rows:pair, rows:] * scale - new[:, rows:])
+                total = jnp.sum(early, axis=0, keepdims=True)
+                total = jnp.concatenate([total[:, :rows], total[:, rows:] + jnp.sum(late, axis=0, keepdims=True)], axis=1)
+                probs = jnp.concatenate([early, jnp.concatenate([jnp.zeros_like(late), late], axis=1)], axis=0)
+            else:
+                probs = jnp.exp2(s_v[i, :span] * scale - new)
+                total = jnp.sum(probs, axis=0, keepdims=True)
             mixed = jnp.dot(vals, probs.astype(BF16), preferred_element_type=F32)
             if diagonal:
                 l_v[i] = total
@@ -243,66 +288,70 @@
         for g in range(group):
             mix(g, tops[g])
 
-    def project_out(o_ref, i):
+    def project_out(parts, fresh):
         for n in range(feats // ocols):
             cols = slice(n * ocols, (n + 1) * ocols)
-            y_v[:, cols] += jnp.dot(o_ref[...], wo_v[i, :, cols], preferred_element_type=F32)
-
-    y_v[...] = jnp.zeros_like(y_v)
-
-    def one_step(idx, _):
-        swap = lax.div(c, CHIPS - 1) * lax.rem(lax.div(idx + 2, 4), 2)
-        t = (1 - swap) * lax.div(idx, 2) + swap * (1 + lax.rem(idx, 2))
-        j = (1 - swap) * lax.rem(idx, 2) + swap * (lax.div(idx, 2) - 1)
-
-        @pl.when(t == 0)
+            total = sum(jnp.dot(o_ref[...], wo_v[i, :, cols], preferred_element_type=F32) for o_ref, i in parts)
+            y_v[:, cols] = total if fresh else y_v[:, cols] + total
+
+    for j in range(halves):
+        kv_wait(j, mate)
+    send_rest(1)
+    finish_q(n_wq - 1)
+    for j in range(halves):
+        attend(j, [c], True)
+
+    relay_now(1, slice(0, 2))
+
+    block = c - lax.div(c, 2) - 1
+
+    def one_half(j, _):
+        @pl.when(third)
         def _():
-            kv_wait(j, mate)
-            attend(j, c, True)
-
-        @pl.when(t > 0)
+            kv_wait(j, 3)
+            attend(j, [c - 1], False)
+
+            @pl.when(j == 0)
+            def _():
+                kv_wait(1, 2)
+                relay(1, 2, 0, up).start()
+
+        @pl.when(last)
         def _():
-            block = c - t + lax.div(c, CHIPS - 1) * lax.div(t, 2) * (2 * lax.rem(t, 2) - 1)
-
-            @pl.when(jnp.logical_or(jnp.logical_not(last), t != 2))
-            def _():
-                for core in range(CORES):
-                    kv_wait(j, block * CORES + core)
-
-            @pl.when(jnp.logical_and(c == 2, t == 1))
-            def _():
-                relay(j, CORES, 0, up).start()
-
-            @pl.when(jnp.logical_and(last, idx == halves + 1))
-            def _():
-                relay_first(1)
-
-            attend(j, block, False)
-
-        @pl.when(t == c)
+            for piece in (4, 5, 0):
+                kv_wait(j, piece)
+            attend(j, [c - 1, 0], False)
+
+            @pl.when(j == 0)
+            def _():
+                kv_wait(1, 1)
+                relay(1, 1, 0, down).start()
+
+        for chip, pieces in ((1, (1,)), (2, (0, 1)), (3, (2, 3))):
+            @pl.when(c == chip)
+            def _():
+                for piece in pieces:
+                    kv_wait(j, piece)
+
+        @pl.when(c > 0)
         def _():
-            for g in range(group):
-                i = j * group + g
-                o = acc_v[i] * (1.0 / l_v[i])
-                for core in range(CORES):
-                    oo_v[j, core, :, g * head:(g + 1) * head] = o[:, core * rows:(core + 1) * rows].T.astype(BF16)
-            o_copy(j).start()
-            i = CORES * j + s
-            pltpu.make_async_copy(wo_hbm.at[pl.ds(0, width)], wo_v.at[i], wo_sem.at[i]).wait()
-            project_out(oo_v.at[j, s], i)
-
+            attend(j, [block], False)
+
+        for g in range(group):
+            i = j * group + g
+            o = acc_v[i] * (1.0 / l_v[i])
+            for core in range(CORES):
+                oo_v[j, core, :, g * head:(g + 1) * head] = o[:, core * rows:(core + 1) * rows].T.astype(BF16)
+        o_copy(j).start()
         return 0
 
-    lax.fori_loop(0, halves * (c + 1), one_step, 0)
-
-    def theirs_out(j, _):
-        i = CORES * j + 1 - s
-        o_copy(j).wait_recv()
-        pltpu.make_async_copy(wo_hbm.at[pl.ds(0, width)], wo_v.at[i], wo_sem.at[i]).wait()
-        project_out(or_v.at[j], i)
-        return 0
-
-    lax.fori_loop(0, halves, theirs_out, 0)
+    lax.fori_loop(0, halves, one_half, 0)
+    for i in range(n_wo):
+        wo_load(i).wait()
+    o_copy(0).wait_recv()
+    project_out(((oo_v.at[0, s], s), (or_v.at[0], 1 - s), (oo_v.at[1, s], CORES + s)), True)
+    o_copy(1).wait_recv()
+    project_out(((or_v.at[1], CORES + 1 - s),), False)
 
     h_copy.wait_send()
     for j in range(halves):
@@ -317,17 +366,10 @@
             def _():
                 to_down(j, core).wait_send()
 
-            @pl.when(last)
-            def _():
-                relay(j, core, core, down).wait_send()
-
-        @pl.when(first)
-        def _():
-            relay(j, 2 * CORES - 1, 0, down).wait_send()
-
-        @pl.when(c == 2)
-        def _():
-            relay(j, CORES, 0, up).wait_send()
+        for chip, block, to in routes:
+            @pl.when(c == chip)
+            def _():
+                relay(j, block, 0, to).wait_send()
 
 
 def solution(mesh):
@@ -343,7 +385,7 @@
         group = q_heads // kv_heads
         width = group * head
         pair = CORES * rows
-        qcols = 512
+        qcols = width
         n_wq = halves * width // qcols
         tables = np.stack(rope_tables(group_size * rows, head))
         by_device = tables.reshape(2, group_size, rows, head).transpose(1, 0, 2, 3)
@@ -365,7 +407,7 @@
             pltpu.VMEM((halves, group_size, 2, rows, head), BF16),
             pltpu.VMEM((2, pair, qcols), F32),
             pltpu.VMEM((halves * group, head, pair), BF16),
-            pltpu.VMEM((halves * group, pair, pair), F32),
+            pltpu.VMEM((halves * group, 2 * pair, pair), F32),
             pltpu.VMEM((halves * group, head, pair), F32),
             pltpu.VMEM((halves * group, 1, pair), F32),
             pltpu.VMEM((halves * group, 1, pair), F32),

time: 21.2 us -> 19.1 us (0.901)
  Pallas kernels: 20.2 us -> 18.1 us
    pallas_call x1, Pallas kernels: 20.2 us -> 18.1 us  [device_step(): pl.pallas_call(kernel, out_shape=pltpu.VMEM((rows, feats), F32), in_specs...]
where the time goes in v3:
time: 19.1 us; the launch traced here: 19 us
  Pallas kernels  18.1 us (95%)
  other arithmetic  0.9 us (5%)
    pallas_call x1, Pallas kernels, device_step(): pl.pallas_call(kernel, out_shape=pltpu.VMEM((rows, feats), F32), in_specs...  18.1 us
    convert_element_type x1, other arithmetic, device_step(): return (hidden.astype(F32) + mixed).astype(BF16)  0.9 us

profile of v3, /device:TPU:87, one launch (start us, length us, event | category | flops | bytes accessed | tf_op | source)
XLA Modules:
  0.0 19.0 jit_solution(1481675004533731705)
XLA Ops:
  0.0 0.0 copy-start
  0.0 18.1 %attention_block.1 = f32[128,2048]{1,0:T(8,128)S(1)} custom-call(bf16[128,2048]{1,0:T(8,128)(2,1)} %x_hbm.1, bf16[16,128]{1,0:T(8,128)(2,1)} %bitcast.3, bf16[2048,4096]{1,0:T(8,128)(2,1)} %wq_hbm.1, bf16[2048,512]{1,0:T(8,128)(2,1)} %wk_hbm.1, bf16[2048,512]{1,0:T(8,128)(2,1)} %wv_hbm.1, bf16[4096,2048]{1,0:T(8,128)(2,1)} %wo_hbm.1, ...), custom_call_target="tpu_custom_call" | custom-call | tf_op jit(solution)/shard_map/attention_block/pallas_call | solution.py:420
  18.1 0.0 copy-done
  18.1 0.9 %add_convert_fusion = bf16[128,2048]{1,0:T(8,128)(2,1)} fusion(f32[128,2048]{1,0:T(8,128)S(1)} %attention_block.1, bf16[128,2048]{1,0:T(8,128)(2,1)S(1)} %copy-done), kind=kLoop, calls=%fused_computation | loop fusion | flops 786432 | bytes 2097152 | tf_op jit(solution)/shard_map/convert_element_type | solution.py:432
Async XLA Ops:
  0.0 18.1 %copy-start = (bf16[128,2048]{1,0:T(8,128)(2,1)S(1)}, bf16[128,2048]{1,0:T(8,128)(2,1)}, u32[]{:S(2)}) copy-start(bf16[128,2048]{1,0:T(8,128)(2,1)} %x_hbm.1) | copy-start | bytes 1572868

commit v4 on v3

--- a/solution.py
+++ b/solution.py
@@ -26,10 +26,10 @@
     return np.concatenate([cos, cos], axis=1), np.concatenate([-sin, sin], axis=1)
 
 
-def kernel(x_hbm, ln_hbm, wq_hbm, wk_hbm, wv_hbm, wo_hbm, qg_hbm, kg_hbm, rope_hbm, ropet_hbm, y_v,
+def kernel(x_hbm, ln_hbm, wq_hbm, wk_hbm, wv_hbm, wo_hbm, qg_hbm, kg_hbm, rope_hbm, ropet_hbm, out_v,
            x_v, ln_v, qg_v, kg_v, rope_v, ropet_v, wkv_v, wq_v, wo_v, h_v, pk_v, kv_v, raw_v, q_v, s_v, acc_v, m_v, l_v,
-           oo_v, or_v,
-           ld_sem, wkv_sem, wq_sem, wo_sem, h_sem, kvp_sem, kvu_sem, kvd_sem, rel_sem, kv_sem, o_sem):
+           oo_v, or_v, y_v,
+           ld_sem, wkv_sem, wq_sem, wo_sem, h_sem, send_sem, kv_sem, o_sem):
     rows, feats = x_v.shape[1], x_v.shape[2]
     head = rope_v.shape[-1]
     pair = CORES * rows
@@ -66,20 +66,24 @@
 
     def wkv_load(j, which):
         src = (wk_hbm, wv_hbm)[which]
-        return pltpu.make_async_copy(src.at[:, pl.ds(j * kvw, kvw)], wkv_v.at[j, :, pl.ds(which * kvw, kvw)], wkv_sem.at[j, which])
+        return pltpu.make_async_copy(src.at[:, pl.ds(j * kvw, kvw)], wkv_v.at[j, :, pl.ds(which * kvw, kvw)], wkv_sem.at[j])
+
+    halfq = qcols // 2
 
     def wq_load(i):
-        j, part = divmod(i, qparts)
-        col = (CORES * j + s) * width + part * qcols
-        return pltpu.make_async_copy(wq_hbm.at[:, pl.ds(pl.multiple_of(col, qcols), qcols)], wq_v.at[i], wq_sem.at[i])
-
-    def wo_load(i):
-        return pltpu.make_async_copy(wo_hbm.at[pl.ds(i * width, width)], wo_v.at[i], wo_sem.at[i])
+        if i < 2:
+            col = s * width + i * halfq
+            return pltpu.make_async_copy(wq_hbm.at[:, pl.ds(pl.multiple_of(col, halfq), halfq)], wq_v.at[0, :, pl.ds(i * halfq, halfq)], wq_sem.at[i])
+        col = (CORES * (i - 1) + s) * width
+        return pltpu.make_async_copy(wq_hbm.at[:, pl.ds(pl.multiple_of(col, qcols), qcols)], wq_v.at[i - 1], wq_sem.at[i])
+
+    def wo_load(i, sem):
+        return pltpu.make_async_copy(wo_hbm.at[pl.ds(pl.multiple_of(i * width, width), width)], wo_v.at[i], sem)
 
     n_wq = halves * qparts
     n_wo = CORES * halves
     stages = [wkv_load(j, which) for j in range(halves) for which in range(2)]
-    for load in loads[:5] + stages:
+    for load in loads[:5] + stages[:2]:
         load.start()
 
     barrier = pltpu.get_barrier_semaphore()
@@ -94,22 +98,25 @@
     h_copy = remote(h_v.at[s], h_v.at[s], h_sem.at[0], h_sem.at[1], (dp, mate))
 
     def to_mate(j):
-        return remote(pk_v.at[j, 1 - s], kv_v.at[j, mine], kvp_sem.at[j], kv_sem.at[j, mine], (dp, mate))
+        return remote(pk_v.at[j, 1 - s], kv_v.at[j, mine], send_sem.at[0], kv_sem.at[j, mine], (dp, mate))
 
     def to_up(j, core):
-        return remote(pk_v.at[j, core], kv_v.at[j, mine], kvu_sem.at[j, core], kv_sem.at[j, mine], dev(up, core))
+        return remote(pk_v.at[j, core], kv_v.at[j, mine], send_sem.at[1], kv_sem.at[j, mine], dev(up, core))
 
     def to_down(j, core):
-        return remote(pk_v.at[j, core], kv_v.at[j, mine], kvd_sem.at[j, core], kv_sem.at[j, mine], dev(down, core))
-
-    def relay(j, block, slot, chip):
-        return remote(kv_v.at[j, block], kv_v.at[j, block], rel_sem.at[j, slot], kv_sem.at[j, block], dev(chip, s))
+        return remote(pk_v.at[j, core], kv_v.at[j, mine], send_sem.at[2], kv_sem.at[j, mine], dev(down, core))
+
+    def relay(j, block, chip):
+        return remote(kv_v.at[j, block], kv_v.at[j, block], send_sem.at[3], kv_sem.at[j, block], dev(chip, s))
 
     def kv_wait(j, block):
-        remote(kv_v.at[j, block], kv_v.at[j, block], kvp_sem.at[0], kv_sem.at[j, block], (dp, mate)).wait_recv()
-
-    def o_copy(j):
-        return remote(oo_v.at[j, 1 - s], or_v.at[j], o_sem.at[0, j], o_sem.at[1, j], (dp, mate))
+        remote(kv_v.at[j, block], kv_v.at[j, block], send_sem.at[0], kv_sem.at[j, block], (dp, mate)).wait_recv()
+
+    def o_copy(j, part=None):
+        theirs = 1 - s
+        if part is None:
+            return remote(oo_v.at[j, theirs], or_v.at[j], o_sem.at[0], o_sem.at[1 + j], (dp, mate))
+        return remote(oo_v.at[j, theirs, part], or_v.at[j, part], o_sem.at[0], o_sem.at[1 + j], (dp, mate))
 
     sends_down = jnp.logical_or(first, jnp.logical_and(c == 1, s == 1))
     second = c == 1
@@ -126,12 +133,12 @@
             @pl.when(c == chip)
             def _():
                 kv_wait(j, block)
-                relay(j, block, 0, to).start()
+                relay(j, block, to).start()
 
     loads[0].wait()
     loads[1].wait()
-    loads[5].start()
-    wq_load(0).start()
+    for load in stages[2:]:
+        load.start()
     gain = jnp.concatenate([ln_v[k:k + 1, :] for k in range(feats // head)], axis=1).astype(F32)
     step = 64
 
@@ -142,6 +149,8 @@
         return 0
 
     lax.fori_loop(0, rows // step, norm_rows, 0)
+    wq_load(0).start()
+    loads[5].start()
     pl.semaphore_wait(barrier, 1 + 2 * CORES)
     h_copy.start()
     for load in loads[2:5]:
@@ -192,13 +201,13 @@
             send(jnp.logical_or(both(second, odd), both(third, odd)), (send_up, 1))
 
     for j in range(halves):
-        wkv_load(j, 0).wait()
-        wkv_load(j, 1).wait()
+        pltpu.make_async_copy(wkv_v.at[j], wkv_v.at[j], wkv_sem.at[j]).wait()
+        if j == 0:
+            wq_load(1).start()
         raw_v[j, :rows, :2 * kvw] = jnp.dot(h_v[s], wkv_v[j], preferred_element_type=F32)
         finish_kv(j)
         if j == 0:
-            for i in range(1, n_wq):
-                wq_load(i).start()
+            wq_load(2).start()
         send_kv(j)
 
     h_copy.wait_recv()
@@ -219,20 +228,24 @@
             t = t * lax.rsqrt(jnp.mean(t * t, axis=0, keepdims=True) + EPS)
             q_v[i * (qcols // head) + g] = (t * ropet_v[0] + turn(t) * ropet_v[1]).astype(BF16)
 
-    for i in range(n_wq):
+    for i in range(2):
         wq_load(i).wait()
-        if i == n_wq - 1:
-            for n in range(n_wo):
-                wo_load(n).start()
-        raw_v[i % 2] = jnp.dot(h_v[...].reshape(pair, feats), wq_v[i], preferred_element_type=F32)
-        if i:
-            finish_q(i - 1)
-        if i + 1 < n_wq:
-            send_rest(0)
-    def attend(j, blocks, diagonal):
-        keys = [kv_v[j, pl.ds(block * CORES, CORES), 0].reshape(pair, head) for block in blocks]
-        vals = jnp.concatenate([kv_v[j, block * CORES + core, 1] for block in blocks for core in range(CORES)], axis=1)
-        span = len(blocks) * pair
+        cols = slice(i * halfq, (i + 1) * halfq)
+        raw_v[0, :, cols] = jnp.dot(h_v[...].reshape(pair, feats), wq_v[0, :, cols], preferred_element_type=F32)
+    send_rest(0)
+    for i in range(1, n_wq):
+        wq_load(i + 1).wait()
+        wo_load(s, wo_sem.at[0]).start()
+        for n in (1 - s, CORES + s, CORES + 1 - s):
+            wo_load(n, wo_sem.at[1]).start()
+        raw_v[i] = jnp.dot(h_v[...].reshape(pair, feats), wq_v[i], preferred_element_type=F32)
+        finish_q(i - 1)
+
+    def attend(j, pieces, diagonal):
+        keys = [kv_v[j, piece, 0] for piece in pieces]
+        keys = [jnp.concatenate(keys[n:n + CORES], axis=0) for n in range(0, len(pieces), CORES)]
+        vals = jnp.concatenate([kv_v[j, piece, 1] for piece in pieces], axis=1)
+        span = len(pieces) * rows
         if diagonal:
             key = lax.broadcasted_iota(jnp.int32, (rows, rows), 0)
             row = lax.broadcasted_iota(jnp.int32, (rows, rows), 1)
@@ -253,7 +266,7 @@
                 top = jnp.max(early, axis=0, keepdims=True)
                 both = jnp.maximum(top[:, rows:], jnp.max(late, axis=0, keepdims=True))
                 return jnp.concatenate([top[:, :rows], both], axis=1) * scale
-            for n in range(len(blocks)):
+            for n in range(len(keys)):
                 sc = jnp.dot(keys[n], q_v[i], preferred_element_type=F32)
                 s_v[i, n * pair:(n + 1) * pair] = sc
                 best = jnp.max(sc, axis=0, keepdims=True) * scale
@@ -288,88 +301,95 @@
         for g in range(group):
             mix(g, tops[g])
 
-    def project_out(parts, fresh):
-        for n in range(feats // ocols):
-            cols = slice(n * ocols, (n + 1) * ocols)
-            total = sum(jnp.dot(o_ref[...], wo_v[i, :, cols], preferred_element_type=F32) for o_ref, i in parts)
-            y_v[:, cols] = total if fresh else y_v[:, cols] + total
+    def project(part, cols):
+        o_ref, i = part
+        return jnp.dot(jnp.concatenate([o_ref[0], o_ref[1]], axis=1), wo_v[i, :, cols], preferred_element_type=F32)
 
     for j in range(halves):
         kv_wait(j, mate)
     send_rest(1)
     finish_q(n_wq - 1)
     for j in range(halves):
-        attend(j, [c], True)
+        attend(j, [c * CORES, c * CORES + 1], True)
 
     relay_now(1, slice(0, 2))
 
-    block = c - lax.div(c, 2) - 1
-
-    def one_half(j, _):
-        @pl.when(third)
-        def _():
-            kv_wait(j, 3)
-            attend(j, [c - 1], False)
-
-            @pl.when(j == 0)
-            def _():
-                kv_wait(1, 2)
-                relay(1, 2, 0, up).start()
-
-        @pl.when(last)
-        def _():
-            for piece in (4, 5, 0):
-                kv_wait(j, piece)
-            attend(j, [c - 1, 0], False)
-
-            @pl.when(j == 0)
-            def _():
-                kv_wait(1, 1)
-                relay(1, 1, 0, down).start()
-
-        for chip, pieces in ((1, (1,)), (2, (0, 1)), (3, (2, 3))):
-            @pl.when(c == chip)
-            def _():
-                for piece in pieces:
-                    kv_wait(j, piece)
-
-        @pl.when(c > 0)
-        def _():
-            attend(j, [block], False)
-
-        for g in range(group):
-            i = j * group + g
-            o = acc_v[i] * (1.0 / l_v[i])
-            for core in range(CORES):
-                oo_v[j, core, :, g * head:(g + 1) * head] = o[:, core * rows:(core + 1) * rows].T.astype(BF16)
-        o_copy(j).start()
+    @pl.when(last)
+    def _():
+        for piece in (4, 5, 0):
+            kv_wait(0, piece)
+        attend(0, (4, 5, 0, 1), False)
+        kv_wait(1, 1)
+        relay(1, 1, down).start()
+
+    def one_step(n, _):
+        is3 = lax.div(c, 3)
+        is2 = lax.div(c, 2) - is3
+        half = lax.div(n, 2)
+        odd_step = lax.rem(n, 2)
+        even_step = 1 - odd_step
+        j = half + is3 * lax.div(3 - n, 3)
+        piece0 = is3 * (even_step * (4 + half) + odd_step * 2) + is2 * 2 * even_step
+        piece1 = is3 * (even_step * (1 - half) + odd_step * 3) + is2 * (2 * even_step + 1) + (1 - is3 - is2)
+
+        @pl.when(jnp.logical_or(both(third, n % 2 == 1), last))
+        def _():
+            kv_wait(j, piece0)
+
+        @pl.when(jnp.logical_or(jnp.logical_or(both(second, n % 2 == 1), third), both(last, n > 0)))
+        def _():
+            kv_wait(j, piece1)
+
+        @pl.when(jnp.logical_or(c > 1, both(second, n % 2 == 1)))
+        def _():
+            attend(j, (piece0, piece1), False)
+
+        @pl.when(both(third, n == 0))
+        def _():
+            kv_wait(1, 2)
+            relay(1, 2, up).start()
+
+        @pl.when(n % 2 == 1)
+        def _():
+            for part in range(2):
+                for g in range(group // 2):
+                    i = half * group + part * (group // 2) + g
+                    o = acc_v[i] * (1.0 / l_v[i])
+                    for core in range(CORES):
+                        oo_v[half, core, part, :, g * head:(g + 1) * head] = o[:, core * rows:(core + 1) * rows].T.astype(BF16)
+                o_copy(half, part).start()
+
+        @pl.when(n == 1)
+        def _():
+            wo_load(s, wo_sem.at[0]).wait()
+            for k in range(feats // ocols):
+                cols = slice(k * ocols, (k + 1) * ocols)
+                y_v[:, cols] = x_v[0, :, cols].astype(F32) + project((oo_v.at[0, s], s), cols)
+
         return 0
 
-    lax.fori_loop(0, halves, one_half, 0)
-    for i in range(n_wo):
-        wo_load(i).wait()
+    lax.fori_loop(0, 2 * halves, one_step, 0)
+    pltpu.make_async_copy(wo_v.at[pl.ds(1, n_wo - 1)], wo_v.at[pl.ds(1, n_wo - 1)], wo_sem.at[1]).wait()
     o_copy(0).wait_recv()
-    project_out(((oo_v.at[0, s], s), (or_v.at[0], 1 - s), (oo_v.at[1, s], CORES + s)), True)
+    for k in range(feats // ocols):
+        cols = slice(k * ocols, (k + 1) * ocols)
+        y_v[:, cols] += project((or_v.at[0], 1 - s), cols) + project((oo_v.at[1, s], CORES + s), cols)
     o_copy(1).wait_recv()
-    project_out(((or_v.at[1], CORES + 1 - s),), False)
+    for k in range(feats // ocols):
+        cols = slice(k * ocols, (k + 1) * ocols)
+        out_v[:, cols] = (y_v[:, cols] + project((or_v.at[1], CORES + 1 - s), cols)).astype(BF16)
 
     h_copy.wait_send()
-    for j in range(halves):
-        to_mate(j).wait_send()
-        o_copy(j).wait_send()
-        for core in range(CORES):
-            @pl.when(jnp.logical_not(last))
-            def _():
-                to_up(j, core).wait_send()
-
-            @pl.when(sends_down)
-            def _():
-                to_down(j, core).wait_send()
-
-        for chip, block, to in routes:
-            @pl.when(c == chip)
-            def _():
-                relay(j, block, 0, to).wait_send()
+    theirs = 1 - s
+    remote(pk_v.at[:, theirs], kv_v.at[:, mine], send_sem.at[0], kv_sem.at[0, 0], (dp, mate)).wait_send()
+    remote(oo_v.at[:, theirs], or_v, o_sem.at[0], o_sem.at[1], (dp, mate)).wait_send()
+
+    def sent(sem):
+        remote(pk_v, kv_v.at[:, pl.ds(0, CORES)], sem, kv_sem.at[0, 0], (dp, mate)).wait_send()
+
+    pl.when(jnp.logical_not(last))(functools.partial(sent, send_sem.at[1]))
+    pl.when(sends_down)(functools.partial(sent, send_sem.at[2]))
+    remote(kv_v.at[:, 0], kv_v.at[:, 0], send_sem.at[3], kv_sem.at[0, 0], (dp, mate)).wait_send()
 
 
 def solution(mesh):
@@ -411,15 +431,14 @@
             pltpu.VMEM((halves * group, head, pair), F32),
             pltpu.VMEM((halves * group, 1, pair), F32),
             pltpu.VMEM((halves * group, 1, pair), F32),
-            pltpu.VMEM((halves, CORES, rows, width), BF16),
-            pltpu.VMEM((halves, rows, width), BF16),
-            dma((6,)), dma((halves, 2)), dma((n_wq,)), dma((kv_heads,)), dma((2,)),
-            dma((halves,)), dma((halves, CORES)), dma((halves, CORES)), dma((halves, CORES)),
-            dma((halves, group_size)), dma((2, halves)),
+            pltpu.VMEM((halves, CORES, 2, rows, width // 2), BF16),
+            pltpu.VMEM((halves, 2, rows, width // 2), BF16),
+            pltpu.VMEM((rows, feats), F32),
+            dma((6,)), dma((halves,)), dma((n_wq + 1,)), dma((2,)), dma((2,)), dma((4,)), dma((halves, group_size)), dma((1 + halves,)),
         ]
         mixed = pl.pallas_call(
             kernel,
-            out_shape=pltpu.VMEM((rows, feats), F32),
+            out_shape=pltpu.VMEM((rows, feats), BF16),
             in_specs=[any_spec] * 10,
             out_specs=pl.BlockSpec(memory_space=pltpu.VMEM),
             scratch_shapes=scratch,
@@ -429,7 +448,7 @@
             name="attention_block",
         )(hidden, ln_gain.reshape(-1, head), w_q, w_k, w_v, w_o, q_gain.reshape(1, -1), k_gain.reshape(1, -1),
           jnp.asarray(by_device), jnp.asarray(by_chip))
-        return (hidden.astype(F32) + mixed).astype(BF16)
+        return mixed
 
     row_spec = P(('dp', 'sp'), None)
     return jax.shard_map(device_step, mesh=mesh, in_specs=(row_spec, P(), P(), P(), P(), P(), P(), P()), out_specs=row_spec, check_vma=False)

time: 19.1 us -> 18.1 us (0.948)
  Pallas kernels: 18.1 us -> 17.2 us
  other arithmetic: 0.9 us -> 0 us
  local copies, waits for them, and re-layouts: 0.01 us -> 0.8 us
    convert_element_type x1 -> x0, other arithmetic: 0.9 us -> none  [device_step(): return (hidden.astype(F32) + mixed).astype(BF16)]
    pallas_call x1, Pallas kernels: 18.1 us -> 17.2 us  [device_step(): pl.pallas_call(kernel, out_shape=pltpu.VMEM((rows, feats), BF16), in_spec...]
    unnamed x2 -> x1, local copies, waits for them, and re-layouts: 0.01 us -> 0.8 us
where the time goes in v4:
time: 18.1 us; the launch traced here: 18 us
  Pallas kernels  17.2 us (95%)
  local copies, waits for them, and re-layouts  0.8 us (4%)
    pallas_call x1, Pallas kernels, device_step(): pl.pallas_call(kernel, out_shape=pltpu.VMEM((rows, feats), BF16), in_spec...  17.2 us
    unnamed x1, local copies, waits for them, and re-layouts  0.8 us

profile of v4, /device:TPU:87, one launch (start us, length us, event | category | flops | bytes accessed | tf_op | source)
XLA Modules:
  0.0 18.0 jit_solution(15170690373403489553)
XLA Ops:
  0.0 17.2 %attention_block.1 = bf16[128,2048]{1,0:T(8,128)(2,1)S(1)} custom-call(bf16[128,2048]{1,0:T(8,128)(2,1)} %x_hbm.1, bf16[16,128]{1,0:T(8,128)(2,1)} %bitcast.3, bf16[2048,4096]{1,0:T(8,128)(2,1)} %wq_hbm.1, bf16[2048,512]{1,0:T(8,128)(2,1)} %wk_hbm.1, bf16[2048,512]{1,0:T(8,128)(2,1)} %wv_hbm.1, bf16[4096,2048]{1,0:T(8,128)(2,1)} %wo_hbm.1, ...), custom_call_target="tpu_custom_call" | custom-call | tf_op jit(solution)/shard_map/attention_block/pallas_call | solution.py:439
  17.2 0.8 %copy.12 = bf16[128,2048]{1,0:T(8,128)(2,1)} copy(bf16[128,2048]{1,0:T(8,128)(2,1)S(1)} %attention_block.1) | data formatting | bytes 1048576

commit v5 on v4

--- a/solution.py
+++ b/solution.py
@@ -135,10 +135,11 @@
                 kv_wait(j, block)
                 relay(j, block, to).start()
 
-    loads[0].wait()
     loads[1].wait()
     for load in stages[2:]:
         load.start()
+    loads[0].wait()
+    wq_load(0).start()
     gain = jnp.concatenate([ln_v[k:k + 1, :] for k in range(feats // head)], axis=1).astype(F32)
     step = 64
 
@@ -149,7 +150,7 @@
         return 0
 
     lax.fori_loop(0, rows // step, norm_rows, 0)
-    wq_load(0).start()
+    wq_load(1).start()
     loads[5].start()
     pl.semaphore_wait(barrier, 1 + 2 * CORES)
     h_copy.start()
@@ -203,24 +204,15 @@
     for j in range(halves):
         pltpu.make_async_copy(wkv_v.at[j], wkv_v.at[j], wkv_sem.at[j]).wait()
         if j == 0:
-            wq_load(1).start()
+            wq_load(2).start()
         raw_v[j, :rows, :2 * kvw] = jnp.dot(h_v[s], wkv_v[j], preferred_element_type=F32)
         finish_kv(j)
-        if j == 0:
-            wq_load(2).start()
         send_kv(j)
 
     h_copy.wait_recv()
-
-    loads[5].wait()
-    q_gain = jnp.broadcast_to(qg_v[...].astype(F32), (head, head)).T
-    q_gain = jnp.concatenate([q_gain] * CORES, axis=1)
 
     def turn(t):
         return jnp.concatenate([t[head // 2:], t[:head // 2]], axis=0)
-
-    ropet_v[0] = ropet_v[0] * q_gain
-    ropet_v[1] = ropet_v[1] * turn(q_gain)
 
     def finish_q(i):
         for g in range(qcols // head):
@@ -233,6 +225,13 @@
         cols = slice(i * halfq, (i + 1) * halfq)
         raw_v[0, :, cols] = jnp.dot(h_v[...].reshape(pair, feats), wq_v[0, :, cols], preferred_element_type=F32)
     send_rest(0)
+    loads[5].wait()
+    q_gain = jnp.broadcast_to(qg_v[...].astype(F32), (head, head)).T
+    q_gain = jnp.concatenate([q_gain] * CORES, axis=1)
+
+    ropet_v[0] = ropet_v[0] * q_gain
+    ropet_v[1] = ropet_v[1] * turn(q_gain)
+
     for i in range(1, n_wq):
         wq_load(i + 1).wait()
         wo_load(s, wo_sem.at[0]).start()
@@ -349,15 +348,24 @@
             kv_wait(1, 2)
             relay(1, 2, up).start()
 
-        @pl.when(n % 2 == 1)
+        def finish_o(j, heads):
+            for g in heads:
+                i = j * group + g
+                o = acc_v[i] * (1.0 / l_v[i])
+                part, at = divmod(g, group // 2)
+                for core in range(CORES):
+                    oo_v[j, core, part, :, at * head:(at + 1) * head] = o[:, core * rows:(core + 1) * rows].T.astype(BF16)
+
+        @pl.when(n == 1)
+        def _():
+            finish_o(0, range(group))
+            o_copy(0).start()
+
+        @pl.when(n == 2 * halves - 1)
         def _():
             for part in range(2):
-                for g in range(group // 2):
-                    i = half * group + part * (group // 2) + g
-                    o = acc_v[i] * (1.0 / l_v[i])
-                    for core in range(CORES):
-                        oo_v[half, core, part, :, g * head:(g + 1) * head] = o[:, core * rows:(core + 1) * rows].T.astype(BF16)
-                o_copy(half, part).start()
+                finish_o(1, range(part * (group // 2), (part + 1) * (group // 2)))
+                o_copy(1, part).start()
 
         @pl.when(n == 1)
         def _():

time: 18.1 us -> 18 us (level)
  no operation moved by 1% of the time
where the time goes in v5:
time: 18 us; the launch traced here: 17.9 us
  Pallas kernels  17.1 us (95%)
  local copies, waits for them, and re-layouts  0.8 us (4%)
    pallas_call x1, Pallas kernels, device_step(): pl.pallas_call(kernel, out_shape=pltpu.VMEM((rows, feats), BF16), in_spec...  17.1 us
    unnamed x1, local copies, waits for them, and re-layouts  0.8 us

profile of v5, /device:TPU:87, one launch (start us, length us, event | category | flops | bytes accessed | tf_op | source)
XLA Modules:
  0.0 17.9 jit_solution(17185064891830744559)
XLA Ops:
  0.0 17.1 %attention_block.1 = bf16[128,2048]{1,0:T(8,128)(2,1)S(1)} custom-call(bf16[128,2048]{1,0:T(8,128)(2,1)} %x_hbm.1, bf16[16,128]{1,0:T(8,128)(2,1)} %bitcast.3, bf16[2048,4096]{1,0:T(8,128)(2,1)} %wq_hbm.1, bf16[2048,512]{1,0:T(8,128)(2,1)} %wk_hbm.1, bf16[2048,512]{1,0:T(8,128)(2,1)} %wv_hbm.1, bf16[4096,2048]{1,0:T(8,128)(2,1)} %wo_hbm.1, ...), custom_call_target="tpu_custom_call" | custom-call | tf_op jit(solution)/shard_map/attention_block/pallas_call | solution.py:447
  17.1 0.8 %copy.12 = bf16[128,2048]{1,0:T(8,128)(2,1)} copy(bf16[128,2048]{1,0:T(8,128)(2,1)S(1)} %attention_block.1) | data formatting | bytes 1048576

commit v6 on v5

--- a/solution.py
+++ b/solution.py
@@ -29,7 +29,7 @@
 def kernel(x_hbm, ln_hbm, wq_hbm, wk_hbm, wv_hbm, wo_hbm, qg_hbm, kg_hbm, rope_hbm, ropet_hbm, out_v,
            x_v, ln_v, qg_v, kg_v, rope_v, ropet_v, wkv_v, wq_v, wo_v, h_v, pk_v, kv_v, raw_v, q_v, s_v, acc_v, m_v, l_v,
            oo_v, or_v, y_v,
-           ld_sem, wkv_sem, wq_sem, wo_sem, h_sem, send_sem, kv_sem, o_sem):
+           ld_sem, wkv_sem, h_sem, send_sem, kv_sem, o_sem):
     rows, feats = x_v.shape[1], x_v.shape[2]
     head = rope_v.shape[-1]
     pair = CORES * rows
@@ -73,9 +73,9 @@
     def wq_load(i):
         if i < 2:
             col = s * width + i * halfq
-            return pltpu.make_async_copy(wq_hbm.at[:, pl.ds(pl.multiple_of(col, halfq), halfq)], wq_v.at[0, :, pl.ds(i * halfq, halfq)], wq_sem.at[i])
+            return pltpu.make_async_copy(wq_hbm.at[:, pl.ds(pl.multiple_of(col, halfq), halfq)], wq_v.at[0, :, pl.ds(i * halfq, halfq)], ld_sem.at[i])
         col = (CORES * (i - 1) + s) * width
-        return pltpu.make_async_copy(wq_hbm.at[:, pl.ds(pl.multiple_of(col, qcols), qcols)], wq_v.at[i - 1], wq_sem.at[i])
+        return pltpu.make_async_copy(wq_hbm.at[:, pl.ds(pl.multiple_of(col, qcols), qcols)], wq_v.at[i - 1], ld_sem.at[i])
 
     def wo_load(i, sem):
         return pltpu.make_async_copy(wo_hbm.at[pl.ds(pl.multiple_of(i * width, width), width)], wo_v.at[i], sem)
@@ -234,9 +234,9 @@
 
     for i in range(1, n_wq):
         wq_load(i + 1).wait()
-        wo_load(s, wo_sem.at[0]).start()
+        wo_load(s, wkv_sem.at[0]).start()
         for n in (1 - s, CORES + s, CORES + 1 - s):
-            wo_load(n, wo_sem.at[1]).start()
+            wo_load(n, wkv_sem.at[1]).start()
         raw_v[i] = jnp.dot(h_v[...].reshape(pair, feats), wq_v[i], preferred_element_type=F32)
         finish_q(i - 1)
 
@@ -369,7 +369,7 @@
 
         @pl.when(n == 1)
         def _():
-            wo_load(s, wo_sem.at[0]).wait()
+            wo_load(s, wkv_sem.at[0]).wait()
             for k in range(feats // ocols):
                 cols = slice(k * ocols, (k + 1) * ocols)
                 y_v[:, cols] = x_v[0, :, cols].astype(F32) + project((oo_v.at[0, s], s), cols)
@@ -377,7 +377,7 @@
         return 0
 
     lax.fori_loop(0, 2 * halves, one_step, 0)
-    pltpu.make_async_copy(wo_v.at[pl.ds(1, n_wo - 1)], wo_v.at[pl.ds(1, n_wo - 1)], wo_sem.at[1]).wait()
+    pltpu.make_async_copy(wo_v.at[pl.ds(1, n_wo - 1)], wo_v.at[pl.ds(1, n_wo - 1)], wkv_sem.at[1]).wait()
     o_copy(0).wait_recv()
     for k in range(feats // ocols):
         cols = slice(k * ocols, (k + 1) * ocols)
@@ -442,7 +442,7 @@
             pltpu.VMEM((halves, CORES, 2, rows, width // 2), BF16),
             pltpu.VMEM((halves, 2, rows, width // 2), BF16),
             pltpu.VMEM((rows, feats), F32),
-            dma((6,)), dma((halves,)), dma((n_wq + 1,)), dma((2,)), dma((2,)), dma((4,)), dma((halves, group_size)), dma((1 + halves,)),
+            dma((6,)), dma((halves,)), dma((2,)), dma((4,)), dma((halves, group_size)), dma((1 + halves,)),
         ]
         mixed = pl.pallas_call(
             kernel,

time: 18 us -> 17.9 us (level)
  no operation moved by 1% of the time
where the time goes in v6:
time: 17.9 us; the launch traced here: 17.8 us
  Pallas kernels  17 us (95%)
  local copies, waits for them, and re-layouts  0.8 us (4%)
    pallas_call x1, Pallas kernels, device_step(): pl.pallas_call(kernel, out_shape=pltpu.VMEM((rows, feats), BF16), in_spec...  17 us
    unnamed x1, local copies, waits for them, and re-layouts  0.8 us

profile of v6, /device:TPU:87, one launch (start us, length us, event | category | flops | bytes accessed | tf_op | source)
XLA Modules:
  0.0 17.8 jit_solution(4483790842569121440)
XLA Ops:
  0.0 17.0 %attention_block.1 = bf16[128,2048]{1,0:T(8,128)(2,1)S(1)} custom-call(bf16[128,2048]{1,0:T(8,128)(2,1)} %x_hbm.1, bf16[16,128]{1,0:T(8,128)(2,1)} %bitcast.3, bf16[2048,4096]{1,0:T(8,128)(2,1)} %wq_hbm.1, bf16[2048,512]{1,0:T(8,128)(2,1)} %wk_hbm.1, bf16[2048,512]{1,0:T(8,128)(2,1)} %wv_hbm.1, bf16[4096,2048]{1,0:T(8,128)(2,1)} %wo_hbm.1, ...), custom_call_target="tpu_custom_call" | custom-call | tf_op jit(solution)/shard_map/attention_block/pallas_call | solution.py:447
  17.0 0.8 %copy.12 = bf16[128,2048]{1,0:T(8,128)(2,1)} copy(bf16[128,2048]{1,0:T(8,128)(2,1)S(1)} %attention_block.1) | data formatting | bytes 1048576
